TPU v7x, 8 devices: a whole 2x2x1 slice. The times are simulated.
8 devices in a mesh: pairs: 1 (over z), cols: 2 (over y), rows: 4 (over x, core).
Axes of the slice: x: 2, y: 2, z: 1, core: 2. Of those that a mesh axis runs over, the one named last changes fastest.
Arguments:
- C1: float32 [3072, 3072], P(('pairs', 'rows'), 'cols')
- C2: float32 [8192, 8192], P(('pairs', 'rows'), 'cols')
- T0: float32 [3072, 8192], P(('pairs', 'rows'), 'cols')
- p: float32 [3072], P(('pairs', 'rows'))
- q: float32 [8192], P(('pairs', 'cols'))
- eps: float32 [8], P('pairs')
Outputs:
- output 1: float32 [3072, 8192], P(('pairs', 'rows'), 'cols')
- output 2: float32 [1], P('pairs')
All inputs are finite; a program needn't handle non-finite values.
Results may differ from a plain program's by a relative error of at most 0.001.
Values are sent between devices in bfloat16 or wider.
A program may use at most 1 GiB of HBM per device.

v0:
```python
import jax
import jax.numpy as jnp
from jax import lax
from jax.sharding import PartitionSpec as P

SWEEPS = 10


def solution(mesh):
    grid_spec = P(("pairs", "rows"), "cols")

    def local_fn(c1_blk, c2_blk, t0_blk, p_blk, q_blk, eps_blk):
        col_pos = lax.axis_index("cols")
        row_pos = lax.axis_index("rows")
        c1_width = c1_blk.shape[1]
        c2_height = c2_blk.shape[0]
        p_full = lax.all_gather(p_blk, "rows", tiled=True)
        q_full = lax.all_gather(q_blk, "cols", tiled=True)
        p_piece = lax.dynamic_slice_in_dim(p_full, col_pos * c1_width, c1_width)
        q_piece = lax.dynamic_slice_in_dim(q_full, row_pos * c2_height, c2_height)
        row_term = lax.psum(jnp.sum(c1_blk * c1_blk * p_piece[None, :], axis=1), "cols")
        col_term = lax.psum(jnp.sum(c2_blk * c2_blk * q_piece[:, None], axis=0), "rows")
        const_blk = row_term[:, None] + col_term[None, :]
        c1_panel = lax.all_gather(c1_blk.astype(jnp.bfloat16), "cols", axis=1, tiled=True)
        c2_panel = lax.all_gather(c2_blk.astype(jnp.bfloat16), "rows", axis=0, tiled=True)

        def cost_of(plan_blk):
            plan_panel = lax.all_gather(plan_blk.astype(jnp.bfloat16), "rows", axis=0, tiled=True)
            lead_blk = jnp.dot(c1_panel, plan_panel, preferred_element_type=jnp.float32)
            lead_panel = lax.all_gather(lead_blk.astype(jnp.bfloat16), "cols", axis=1, tiled=True)
            cross_blk = jnp.dot(lead_panel, c2_panel, preferred_element_type=jnp.float32)
            return const_blk - 2.0 * cross_blk

        def balance(kernel):
            def sweep(sweep_idx, scales):
                row_scale = p_blk / lax.psum(jnp.sum(kernel * scales[1][None, :], axis=1), "cols")
                col_scale = q_blk / lax.psum(jnp.sum(kernel * row_scale[:, None], axis=0), "rows")
                return row_scale, col_scale
            row_scale, col_scale = lax.fori_loop(0, SWEEPS, sweep, (jnp.ones_like(p_blk), jnp.ones_like(q_blk)))
            return row_scale[:, None] * kernel * col_scale[None, :]

        plan_blk = t0_blk
        for step_idx in range(eps_blk.shape[0]):
            cost_blk = cost_of(plan_blk)
            row_shift = lax.pmin(jnp.min(cost_blk, axis=1), "cols")
            kernel = jnp.exp(-(cost_blk - row_shift[:, None]) / eps_blk[step_idx])
            plan_blk = balance(kernel)
        cost_blk = cost_of(plan_blk)
        loss_val = lax.psum(jnp.sum(cost_blk * plan_blk), ("rows", "cols"))
        return plan_blk, loss_val.reshape(1)

    return jax.shard_map(local_fn, mesh=mesh, in_specs=(grid_spec, grid_spec, grid_spec, P(("pairs", "rows")), P(("pairs", "cols")), P("pairs")), out_specs=(grid_spec, P("pairs")), check_vma=False)
```

profile of v0, /device:TPU:0, one launch (start us, length us, event | category | flops | bytes accessed | tf_op | source)
XLA Modules:
  0.0 6423.8 jit_solution(7053173854755618075)
XLA Ops:
  84.4 155.0 %all-gather.24.cloned.1.call-done = bf16[3072,4096]{1,0:T(8,128)(2,1)} async-done(((bf16[768,4096]{1,0:T(8,128)(2,1)}), bf16[3072,4096]{1,0:T(8,128)(2,1)}) %all-gather.24.cloned.1.call-update) | async-done | bytes 25165840 | tf_op jit(solution)/shard_map/all_gather | solution.py:28
  415.7 391.1 %all-gather.28.cloned.1.call-done = bf16[8192,4096]{1,0:T(8,128)(2,1)} async-done(((bf16[2048,4096]{1,0:T(8,128)(2,1)}), bf16[8192,4096]{1,0:T(8,128)(2,1)}) %all-gather.28.cloned.1.call-update) | async-done | bytes 67108880 | tf_op jit(solution)/shard_map/all_gather | solution.py:25
  886.8 269.0 %while.104 = (s32[]{:T(128)}, f32[768]{0:T(1024)}, f32[4096]{0:T(1024)S(1)}, f32[768,4096]{1,0:T(8,128)}, f32[768]{0:T(1024)S(1)}, /*index=5*/f32[4096]{0:T(1024)S(1)}, s32[]{:T(128)}, s32[]{:T(128)}) while((s32[]{:T(128)}, f32[768]{0:T(1024)}, f32[4096]{0:T(1024)S(1)}, f32[768,4096]{1,0:T(8,128)}, f32[768]{0:T(1024)S(1)}, ...), condition=%wide.region_11.0_spmd.clone, body=%wide.region_6.0_spmd.clone.sunk | while | flops 12591875 | bytes 25347196 | solution.py:39
  1167.2 153.2 %all-gather.30.cloned.1.call-done = bf16[3072,4096]{1,0:T(8,128)(2,1)} async-done(((bf16[768,4096]{1,0:T(8,128)(2,1)}), bf16[3072,4096]{1,0:T(8,128)(2,1)}) %all-gather.30.cloned.1.call-update) | async-done | bytes 25165840 | tf_op jit(solution)/shard_map/all_gather | solution.py:28
  1576.9 269.0 %while.105 = (s32[]{:T(128)}, f32[768]{0:T(1024)}, f32[4096]{0:T(1024)S(1)}, f32[768,4096]{1,0:T(8,128)}, f32[768]{0:T(1024)S(1)}, /*index=5*/f32[4096]{0:T(1024)S(1)}, s32[]{:T(128)}, s32[]{:T(128)}) while((s32[]{:T(128)}, f32[768]{0:T(1024)}, f32[4096]{0:T(1024)S(1)}, f32[768,4096]{1,0:T(8,128)}, f32[768]{0:T(1024)S(1)}, ...), condition=%wide.region_19.0_spmd.clone, body=%wide.region_14.0_spmd.clone.sunk | while | flops 12591875 | bytes 25347196 | solution.py:39
  1857.6 152.7 %all-gather.34.cloned.1.call-done = bf16[3072,4096]{1,0:T(8,128)(2,1)} async-done(((bf16[768,4096]{1,0:T(8,128)(2,1)}), bf16[3072,4096]{1,0:T(8,128)(2,1)}) %all-gather.34.cloned.1.call-update) | async-done | bytes 25165840 | tf_op jit(solution)/shard_map/all_gather | solution.py:28
  2036.3 150.7 %all-gather.36.cloned.1.call-done = bf16[768,8192]{0,1:T(8,128)(2,1)} async-done(((bf16[768,4096]{0,1:T(8,128)(2,1)}), bf16[768,8192]{0,1:T(8,128)(2,1)}) %all-gather.36.cloned.1.call-update) | async-done | bytes 12582928 | tf_op jit(solution)/shard_map/all_gather | solution.py:30
  2267.1 269.0 %while.106 = (s32[]{:T(128)}, f32[768]{0:T(1024)}, f32[4096]{0:T(1024)S(1)}, f32[768,4096]{1,0:T(8,128)}, f32[768]{0:T(1024)S(1)}, /*index=5*/f32[4096]{0:T(1024)S(1)}, s32[]{:T(128)}, s32[]{:T(128)}) while((s32[]{:T(128)}, f32[768]{0:T(1024)}, f32[4096]{0:T(1024)S(1)}, f32[768,4096]{1,0:T(8,128)}, f32[768]{0:T(1024)S(1)}, ...), condition=%wide.region_27.0_spmd.clone, body=%wide.region_22.0_spmd.clone.sunk | while | flops 12591875 | bytes 25347196 | solution.py:39
  2547.5 153.1 %all-gather.38.cloned.1.call-done = bf16[3072,4096]{1,0:T(8,128)(2,1)} async-done(((bf16[768,4096]{1,0:T(8,128)(2,1)}), bf16[3072,4096]{1,0:T(8,128)(2,1)}) %all-gather.38.cloned.1.call-update) | async-done | bytes 25165840 | tf_op jit(solution)/shard_map/all_gather | solution.py:28
  2957.1 269.0 %while.107 = (s32[]{:T(128)}, f32[768]{0:T(1024)}, f32[4096]{0:T(1024)S(1)}, f32[768,4096]{1,0:T(8,128)}, f32[768]{0:T(1024)S(1)}, /*index=5*/f32[4096]{0:T(1024)S(1)}, s32[]{:T(128)}, s32[]{:T(128)}) while((s32[]{:T(128)}, f32[768]{0:T(1024)}, f32[4096]{0:T(1024)S(1)}, f32[768,4096]{1,0:T(8,128)}, f32[768]{0:T(1024)S(1)}, ...), condition=%wide.region_35.0_spmd.clone, body=%wide.region_30.0_spmd.clone.sunk | while | flops 12591875 | bytes 25347196 | solution.py:39
  3237.9 152.7 %all-gather.42.cloned.1.call-done = bf16[3072,4096]{1,0:T(8,128)(2,1)} async-done(((bf16[768,4096]{1,0:T(8,128)(2,1)}), bf16[3072,4096]{1,0:T(8,128)(2,1)}) %all-gather.42.cloned.1.call-update) | async-done | bytes 25165840 | tf_op jit(solution)/shard_map/all_gather | solution.py:28
  3416.5 150.7 %all-gather.44.cloned.1.call-done = bf16[768,8192]{0,1:T(8,128)(2,1)} async-done(((bf16[768,4096]{0,1:T(8,128)(2,1)}), bf16[768,8192]{0,1:T(8,128)(2,1)}) %all-gather.44.cloned.1.call-update) | async-done | bytes 12582928 | tf_op jit(solution)/shard_map/all_gather | solution.py:30
  3647.3 269.0 %while.108 = (s32[]{:T(128)}, f32[768]{0:T(1024)}, f32[4096]{0:T(1024)S(1)}, f32[768,4096]{1,0:T(8,128)}, f32[768]{0:T(1024)S(1)}, /*index=5*/f32[4096]{0:T(1024)S(1)}, s32[]{:T(128)}, s32[]{:T(128)}) while((s32[]{:T(128)}, f32[768]{0:T(1024)}, f32[4096]{0:T(1024)S(1)}, f32[768,4096]{1,0:T(8,128)}, f32[768]{0:T(1024)S(1)}, ...), condition=%wide.region_43.0_spmd.clone, body=%wide.region_38.0_spmd.clone.sunk | while | flops 12591875 | bytes 25347196 | solution.py:39
  3927.6 153.1 %all-gather.46.cloned.1.call-done = bf16[3072,4096]{1,0:T(8,128)(2,1)} async-done(((bf16[768,4096]{1,0:T(8,128)(2,1)}), bf16[3072,4096]{1,0:T(8,128)(2,1)}) %all-gather.46.cloned.1.call-update) | async-done | bytes 25165840 | tf_op jit(solution)/shard_map/all_gather | solution.py:28
  4106.9 150.5 %all-gather.48.cloned.1.call-done = bf16[768,8192]{0,1:T(8,128)(2,1)} async-done(((bf16[768,4096]{0,1:T(8,128)(2,1)}), bf16[768,8192]{0,1:T(8,128)(2,1)}) %all-gather.48.cloned.1.call-update) | async-done | bytes 12582928 | tf_op jit(solution)/shard_map/all_gather | solution.py:30
  4337.3 269.0 %while.109 = (s32[]{:T(128)}, f32[768]{0:T(1024)}, f32[4096]{0:T(1024)S(1)}, f32[768,4096]{1,0:T(8,128)}, f32[768]{0:T(1024)S(1)}, /*index=5*/f32[4096]{0:T(1024)S(1)}, s32[]{:T(128)}, s32[]{:T(128)}) while((s32[]{:T(128)}, f32[768]{0:T(1024)}, f32[4096]{0:T(1024)S(1)}, f32[768,4096]{1,0:T(8,128)}, f32[768]{0:T(1024)S(1)}, ...), condition=%wide.region_51.0_spmd.clone, body=%wide.region_46.0_spmd.clone.sunk | while | flops 12591875 | bytes 25347196 | solution.py:39
  4618.0 152.7 %all-gather.50.cloned.1.call-done = bf16[3072,4096]{1,0:T(8,128)(2,1)} async-done(((bf16[768,4096]{1,0:T(8,128)(2,1)}), bf16[3072,4096]{1,0:T(8,128)(2,1)}) %all-gather.50.cloned.1.call-update) | async-done | bytes 25165840 | tf_op jit(solution)/shard_map/all_gather | solution.py:28
  4796.7 150.7 %all-gather.52.cloned.1.call-done = bf16[768,8192]{0,1:T(8,128)(2,1)} async-done(((bf16[768,4096]{0,1:T(8,128)(2,1)}), bf16[768,8192]{0,1:T(8,128)(2,1)}) %all-gather.52.cloned.1.call-update) | async-done | bytes 12582928 | tf_op jit(solution)/shard_map/all_gather | solution.py:30
  5027.5 269.0 %while.110 = (s32[]{:T(128)}, f32[768]{0:T(1024)}, f32[4096]{0:T(1024)S(1)}, f32[768,4096]{1,0:T(8,128)}, f32[768]{0:T(1024)S(1)}, /*index=5*/f32[4096]{0:T(1024)S(1)}, s32[]{:T(128)}, s32[]{:T(128)}) while((s32[]{:T(128)}, f32[768]{0:T(1024)}, f32[4096]{0:T(1024)S(1)}, f32[768,4096]{1,0:T(8,128)}, f32[768]{0:T(1024)S(1)}, ...), condition=%wide.region_59.0_spmd.clone, body=%wide.region_54.0_spmd.clone.sunk | while | flops 12591875 | bytes 25347196 | solution.py:39
  5307.9 153.1 %all-gather.54.cloned.1.call-done = bf16[3072,4096]{1,0:T(8,128)(2,1)} async-done(((bf16[768,4096]{1,0:T(8,128)(2,1)}), bf16[3072,4096]{1,0:T(8,128)(2,1)}) %all-gather.54.cloned.1.call-update) | async-done | bytes 25165840 | tf_op jit(solution)/shard_map/all_gather | solution.py:28
  5487.2 150.5 %all-gather.56.cloned.1.call-done = bf16[768,8192]{0,1:T(8,128)(2,1)} async-done(((bf16[768,4096]{0,1:T(8,128)(2,1)}), bf16[768,8192]{0,1:T(8,128)(2,1)}) %all-gather.56.cloned.1.call-update) | async-done | bytes 12582928 | tf_op jit(solution)/shard_map/all_gather | solution.py:30
  5717.6 269.0 %while.111 = (s32[]{:T(128)}, f32[768]{0:T(1024)}, f32[4096]{0:T(1024)S(1)}, f32[768,4096]{1,0:T(8,128)}, f32[768]{0:T(1024)S(1)}, /*index=5*/f32[4096]{0:T(1024)S(1)}, s32[]{:T(128)}, s32[]{:T(128)}) while((s32[]{:T(128)}, f32[768]{0:T(1024)}, f32[4096]{0:T(1024)S(1)}, f32[768,4096]{1,0:T(8,128)}, f32[768]{0:T(1024)S(1)}, ...), condition=%wide.region_67.0_spmd.clone, body=%wide.region_62.0_spmd.clone.sunk | while | flops 12591875 | bytes 25347196 | solution.py:39
  6001.4 152.8 %all-gather.58.cloned.1.call-done = bf16[3072,4096]{1,0:T(8,128)(2,1)} async-done(((bf16[768,4096]{1,0:T(8,128)(2,1)}), bf16[3072,4096]{1,0:T(8,128)(2,1)}) %all-gather.58.cloned.1.call-update) | async-done | bytes 25165840 | tf_op jit(solution)/shard_map/all_gather | solution.py:28
  6180.2 150.7 %all-gather.60.cloned.1.call-done = bf16[768,8192]{0,1:T(8,128)(2,1)} async-done(((bf16[768,4096]{0,1:T(8,128)(2,1)}), bf16[768,8192]{0,1:T(8,128)(2,1)}) %all-gather.60.cloned.1.call-update) | async-done | bytes 12582928 | tf_op jit(solution)/shard_map/all_gather | solution.py:30
  (840 shorter events, 3733.2 us)
Async XLA Ops:
  7.2 77.2 %all-gather.22.cloned.1.call-start = ((), (), s32[]{:S(2)}) async-start(), calls=%async_computation | async-start | bytes 7077888 | tf_op jit(solution)/shard_map/all_gather | solution.py:24
  24.0 215.4 %all-gather.24.cloned.1.call-start = ((), (), s32[]{:S(2)}) async-start(), calls=%async_computation.1 | async-start | bytes 31457280 | tf_op jit(solution)/shard_map/all_gather | solution.py:28
  32.3 232.6 %copy-start = (f32[4096]{0:T(1024)S(1)}, f32[4096]{0:T(1024)}, u32[]{:S(2)}) copy-start(f32[4096]{0:T(1024)} %param.26) | copy-start | bytes 49156
  32.3 383.4 %all-gather.26.cloned.1.call-start = ((), (), s32[]{:S(2)}) async-start(), calls=%async_computation.2 | async-start | bytes 18874368 | tf_op jit(solution)/shard_map/all_gather | solution.py:30
  264.9 541.9 %all-gather.28.cloned.1.call-start = ((), (), s32[]{:S(2)}) async-start(), calls=%async_computation.3 | async-start | bytes 83886080 | tf_op jit(solution)/shard_map/all_gather | solution.py:25
  298.2 1022.1 %all-gather.30.cloned.1.call-start = ((), (), s32[]{:S(2)}) async-start(), calls=%async_computation.4 | async-start | bytes 31457280 | tf_op jit(solution)/shard_map/all_gather | solution.py:28
  897.3 16.4 copy-start.3
  924.2 16.4 copy-start.3
  951.1 16.4 copy-start.3
  1167.1 329.8 %all-gather.32.cloned.1.call-start = ((), (), s32[]{:S(2)}) async-start(), calls=%async_computation.5 | async-start | bytes 18874368 | tf_op jit(solution)/shard_map/all_gather | solution.py:30
  1346.2 664.1 %all-gather.34.cloned.1.call-start = ((), (), s32[]{:S(2)}) async-start(), calls=%async_computation.6 | async-start | bytes 31457280 | tf_op jit(solution)/shard_map/all_gather | solution.py:28
  1857.2 329.8 %all-gather.36.cloned.1.call-start = ((), (), s32[]{:S(2)}) async-start(), calls=%async_computation.7 | async-start | bytes 18874368 | tf_op jit(solution)/shard_map/all_gather | solution.py:30
  2036.2 664.4 %all-gather.38.cloned.1.call-start = ((), (), s32[]{:S(2)}) async-start(), calls=%async_computation.8 | async-start | bytes 31457280 | tf_op jit(solution)/shard_map/all_gather | solution.py:28
  2547.4 329.8 %all-gather.40.cloned.1.call-start = ((), (), s32[]{:S(2)}) async-start(), calls=%async_computation.9 | async-start | bytes 18874368 | tf_op jit(solution)/shard_map/all_gather | solution.py:30
  2726.4 664.1 %all-gather.42.cloned.1.call-start = ((), (), s32[]{:S(2)}) async-start(), calls=%async_computation.10 | async-start | bytes 31457280 | tf_op jit(solution)/shard_map/all_gather | solution.py:28
  3237.4 329.7 %all-gather.44.cloned.1.call-start = ((), (), s32[]{:S(2)}) async-start(), calls=%async_computation.11 | async-start | bytes 18874368 | tf_op jit(solution)/shard_map/all_gather | solution.py:30
  3416.5 664.3 %all-gather.46.cloned.1.call-start = ((), (), s32[]{:S(2)}) async-start(), calls=%async_computation.12 | async-start | bytes 31457280 | tf_op jit(solution)/shard_map/all_gather | solution.py:28
  3927.6 329.8 %all-gather.48.cloned.1.call-start = ((), (), s32[]{:S(2)}) async-start(), calls=%async_computation.13 | async-start | bytes 18874368 | tf_op jit(solution)/shard_map/all_gather | solution.py:30
  4106.6 664.1 %all-gather.50.cloned.1.call-start = ((), (), s32[]{:S(2)}) async-start(), calls=%async_computation.14 | async-start | bytes 31457280 | tf_op jit(solution)/shard_map/all_gather | solution.py:28
  4617.6 329.7 %all-gather.52.cloned.1.call-start = ((), (), s32[]{:S(2)}) async-start(), calls=%async_computation.15 | async-start | bytes 18874368 | tf_op jit(solution)/shard_map/all_gather | solution.py:30
  4796.6 664.4 %all-gather.54.cloned.1.call-start = ((), (), s32[]{:S(2)}) async-start(), calls=%async_computation.16 | async-start | bytes 31457280 | tf_op jit(solution)/shard_map/all_gather | solution.py:28
  5307.9 329.7 %all-gather.56.cloned.1.call-start = ((), (), s32[]{:S(2)}) async-start(), calls=%async_computation.17 | async-start | bytes 18874368 | tf_op jit(solution)/shard_map/all_gather | solution.py:30
  5486.9 667.4 %all-gather.58.cloned.1.call-start = ((), (), s32[]{:S(2)}) async-start(), calls=%async_computation.18 | async-start | bytes 31457280 | tf_op jit(solution)/shard_map/all_gather | solution.py:28
  6001.1 329.8 %all-gather.60.cloned.1.call-start = ((), (), s32[]{:S(2)}) async-start(), calls=%async_computation.19 | async-start | bytes 18874368 | tf_op jit(solution)/shard_map/all_gather | solution.py:30
  (79 other events, 1288.5 us)
Sparse Core Ops, SparseCore 0:
  24.1 60.2 all-gather.21
  86.5 152.8 all-gather.23
  265.0 150.6 all-gather.25
  417.1 389.6 all-gather.27
  1167.2 153.0 all-gather.29
  1346.3 150.5 all-gather.31
  1857.3 152.9 all-gather.33
  2036.3 150.5 all-gather.35
  2547.5 152.9 all-gather.37
  2726.6 150.5 all-gather.39
  3237.6 152.9 all-gather.41
  3416.6 150.5 all-gather.43
  3927.7 152.9 all-gather.45
  4106.7 150.5 all-gather.47
  4617.7 152.9 all-gather.49
  4796.7 150.5 all-gather.51
  5308.0 152.9 all-gather.53
  5487.0 150.5 all-gather.55
  6001.2 152.9 all-gather.57
  6180.3 150.5 all-gather.59
where the time goes:
time: 6440 us; the launch traced here: 6420 us
  waiting for transfers between devices  3130 us (49%)
  blocking collectives  1300 us (20%)
  other arithmetic  1180 us (18%)
  matrix products  792 us (12%)
    all_gather x9, waiting for transfers between devices, cost_of(): lax.all_gather(plan_blk.astype(jnp.bfloat16), 'rows', axis=0, tiled=True)  1380 us
    all_gather x9, waiting for transfers between devices, cost_of(): lax.all_gather(lead_blk.astype(jnp.bfloat16), 'cols', axis=1, tiled=True)  1310 us
    psum x80, blocking collectives, sweep(): lax.psum(jnp.sum(kernel * row_scale[:, None], axis=0), 'rows')  809 us
    dot_general x9, matrix products, cost_of(): jnp.dot(lead_panel, c2_panel, preferred_element_type=jnp.float32)  560 us
    reduce_sum x80, other arithmetic, sweep(): jnp.sum(kernel * row_scale[:, None], axis=0)  498 us
    reduce_sum x80, other arithmetic, sweep(): jnp.sum(kernel * scales[1][None, :], axis=1)  445 us
    psum x80, blocking collectives, sweep(): lax.psum(jnp.sum(kernel * scales[1][None, :], axis=1), 'cols')  395 us
    all_gather x1, waiting for transfers between devices, local_fn(): lax.all_gather(c2_blk.astype(jnp.bfloat16), 'rows', axis=0, tiled=True)  391 us
  transfers between devices with their start and end apart: 20, of which 20 were waited for; matrix products, arithmetic and copies ran while one was open for 1% of the time, Pallas kernels for 0%

commit v1 on v0

v1 whole, which is shorter than its diff:
```python
import functools

import jax
import jax.numpy as jnp
from jax import lax
from jax.experimental import pallas as pl
from jax.experimental.pallas import tpu as pltpu
from jax.sharding import PartitionSpec as P

SWEEPS = 10
W = 256
AHEAD = 4
RB = 64
LEADS = 4
LANES = 128
SUB = 8
F32 = jnp.float32
BF16 = jnp.bfloat16


def outer_kernel(steps, c1_ref, t0_ref, c2_ref, a_ref, b_ref, p_ref, q_ref, eps_ref, t_out, loss_out,
                 acc, panel, lead, lead_in, c2_own, c2_in, v_ref, r_send, r_in, c_send, c_in, stage,
                 x_send, x_recv, d_send, d_recv, f_send, f_recv, y_send, y_recv,
                 own_sem, in_sem, rs_sem, rr_sem, cs_sem, cr_sem, io_sem, st_sem):
    rows, cols = acc.shape
    chunks = cols // W
    row_at = lax.axis_index("rows")
    col_at = lax.axis_index("cols")
    chip, core = row_at // 2, row_at % 2
    sib = chip * 2 + (1 - core)
    across = (1 - chip) * 2 + core
    diag = (1 - chip) * 2 + (1 - core)
    to_sib, to_across, to_diag, to_col = {"rows": sib}, {"rows": across}, {"rows": diag}, {"cols": 1 - col_at}
    trio = (to_sib, to_across, to_diag)

    barrier = pltpu.get_barrier_semaphore()
    for dev in (*trio, to_col):
        pl.semaphore_signal(barrier, inc=1, device_id=dev)
    pl.semaphore_wait(barrier, 4)

    def rows_of(owner):
        return pl.ds(pl.multiple_of(owner * rows, rows), rows)

    def x_copy(j):
        part = panel.at[j, rows_of(row_at)]
        return pltpu.make_async_remote_copy(part, part, x_send.at[j], x_recv.at[j], device_id=to_across)

    def d_copy(j):
        part = panel.at[j, rows_of(row_at)]
        return pltpu.make_async_remote_copy(part, part, d_send.at[j], d_recv.at[j], device_id=to_sib)

    def f_copy(j):
        part = panel.at[j, rows_of(across)]
        return pltpu.make_async_remote_copy(part, part, f_send.at[j], f_recv.at[j], device_id=to_sib)

    def y_copy(j):
        return pltpu.make_async_remote_copy(lead.at[j % LEADS], lead_in.at[j], y_send.at[j], y_recv.at[j], device_id=to_col)

    def c2_copy(owner, i, buf, sem):
        src = c2_ref.at[pl.ds(pl.multiple_of(owner * cols + i * W, W), W)]
        return pltpu.make_async_copy(src, buf.at[i % 2], sem.at[i % 2])

    def own_copy(i):
        return c2_copy(col_at, i, c2_own, own_sem)

    def in_copy(i):
        return c2_copy(1 - col_at, i, c2_in, in_sem)

    def add_product(left, right, first):
        tile = 512

        def body(n, _):
            at = pl.ds(pl.multiple_of(n * tile, tile), tile)
            prod = jnp.dot(left[...], right[:, at], preferred_element_type=F32)
            if first:
                acc[:, at] = prod
            else:
                acc[:, at] = acc[:, at] + prod
            return 0
        lax.fori_loop(0, cols // tile, body, 0)

    lane = lax.broadcasted_iota(jnp.int32, (SUB, LANES), 1)

    def unpack(packed, g):
        return jnp.sum(jnp.where(lane == g, packed, 0.0), axis=1, keepdims=True)

    def pack(packed, col, g):
        return jnp.where(lane == g, col, packed)

    def lanes(t):
        return slice(t * LANES, (t + 1) * LANES)

    tiles = cols // LANES
    per = RB // SUB
    blocks = rows // RB

    def row_exchange(value, slot, combine):
        r_send[slot] = value
        copy = pltpu.make_async_remote_copy(r_send.at[slot], r_in.at[slot], rs_sem.at[slot], rr_sem.at[slot], device_id=to_col)
        copy.start()
        copy.wait()
        return combine(value, r_in[slot])

    def cost():
        def issue(j, _):
            x_copy(j).start()
            d_copy(j).start()
            return 0
        lax.fori_loop(0, AHEAD, issue, 0)
        for i in range(2):
            own_copy(i).start()
            in_copy(i).start()

        def own_part(i, first):
            own_copy(i).wait()
            add_product(lead.at[i % LEADS], c2_own.at[i % 2], first)

            @pl.when(i + 2 < chunks)
            def _():
                own_copy(i + 2).start()

        def step(j, _):
            @pl.when(j < chunks)
            def _():
                x_copy(j).wait_recv()
                f_copy(j).start()

                @pl.when(j + AHEAD < chunks)
                def _():
                    issue(j + AHEAD, 0)

            @pl.when(j == 1)
            def _():
                own_part(0, True)

            @pl.when((j > 1) & (j <= chunks))
            def _():
                own_part(j - 1, False)

            @pl.when(j < chunks)
            def _():
                d_copy(j).wait_recv()
                f_copy(j).wait_recv()

                @pl.when(j >= LEADS)
                def _():
                    y_copy(j - LEADS).wait_send()
                lead[j % LEADS] = jnp.dot(c1_ref[...], panel[j], preferred_element_type=F32).astype(BF16)
                y_copy(j).start()

            @pl.when(j >= 2)
            def _():
                i = j - 2
                y_copy(i).wait_recv()
                in_copy(i).wait()
                add_product(lead_in.at[i], c2_in.at[i % 2], False)

                @pl.when(i + 2 < chunks)
                def _():
                    in_copy(i + 2).start()
            return 0
        lax.fori_loop(0, chunks + 2, step, 0)

        def drain(j, _):
            x_copy(j).wait_send()
            d_copy(j).wait_send()
            f_copy(j).wait_send()
            return 0
        lax.fori_loop(0, chunks, drain, 0)
        for j in range(chunks - LEADS, chunks):
            y_copy(j).wait_send()

    def cost_min():
        def body(i, packed):
            at = pl.ds(pl.multiple_of(i * RB, RB), RB)
            a_rep = jnp.concatenate([jnp.broadcast_to(unpack(a_ref[...], i * per + k), (SUB, LANES)) for k in range(per)], axis=0)
            low = None
            for t in range(tiles):
                val = (a_rep + b_ref[:, lanes(t)]) - 2.0 * acc[at, lanes(t)]
                acc[at, lanes(t)] = val
                low = val if low is None else jnp.minimum(low, val)
            low = jnp.min(low, axis=1, keepdims=True)
            for k in range(per):
                packed = pack(packed, low[k * SUB:(k + 1) * SUB], i * per + k)
            return packed
        return lax.fori_loop(0, blocks, body, jnp.zeros((SUB, LANES), F32))

    def gibbs(low, scale):
        def body(i, packed):
            at = pl.ds(pl.multiple_of(i * RB, RB), RB)
            low_rep = jnp.concatenate([jnp.broadcast_to(unpack(low, i * per + k), (SUB, LANES)) for k in range(per)], axis=0)
            total = None
            for t in range(tiles):
                val = jnp.exp((low_rep - acc[at, lanes(t)]) * scale)
                acc[at, lanes(t)] = val
                total = val if total is None else total + val
            total = jnp.sum(total, axis=1, keepdims=True)
            for k in range(per):
                packed = pack(packed, total[k * SUB:(k + 1) * SUB], i * per + k)
            return packed
        return lax.fori_loop(0, blocks, body, jnp.ones((SUB, LANES), F32))

    def row_sums():
        def body(i, packed):
            at = pl.ds(pl.multiple_of(i * RB, RB), RB)
            total = None
            for t in range(tiles):
                val = acc[at, lanes(t)] * v_ref[:, lanes(t)]
                total = val if total is None else total + val
            total = jnp.sum(total, axis=1, keepdims=True)
            for k in range(per):
                packed = pack(packed, total[k * SUB:(k + 1) * SUB], i * per + k)
            return packed
        return lax.fori_loop(0, blocks, body, jnp.ones((SUB, LANES), F32))

    def col_sums(u, slot):
        def body(i, sums):
            reps = [jnp.broadcast_to(unpack(u, i * per + k), (SUB, LANES)) for k in range(per)]
            out = []
            for t in range(tiles):
                val = sums[t]
                for k in range(per):
                    val = val + acc[pl.ds(pl.multiple_of(i * RB + k * SUB, SUB), SUB), lanes(t)] * reps[k]
                out.append(val)
            return tuple(out)
        sums = lax.fori_loop(0, blocks, body, tuple(jnp.zeros((SUB, LANES), F32) for _ in range(tiles)))
        for t in range(tiles):
            c_send[slot, :, lanes(t)] = jnp.sum(sums[t], axis=0, keepdims=True)

    def col_update(u, slot):
        col_sums(u, slot)
        copies = [
            pltpu.make_async_remote_copy(c_send.at[slot], c_in.at[slot, n], cs_sem.at[slot, n], cr_sem.at[slot, n], device_id=dev)
            for n, dev in enumerate(trio)
        ]
        for copy in copies:
            copy.start()
        for copy in copies:
            copy.wait()
        v_ref[...] = q_ref[...] / ((c_send[slot] + c_in[slot, 0]) + (c_in[slot, 1] + c_in[slot, 2]))

    def make_plan(u):
        def body(i, _):
            at = pl.ds(pl.multiple_of(i * RB, RB), RB)
            u_rep = jnp.concatenate([jnp.broadcast_to(unpack(u, i * per + k), (SUB, LANES)) for k in range(per)], axis=0)
            for t in range(tiles):
                val = (u_rep * acc[at, lanes(t)]) * v_ref[:, lanes(t)]
                acc[at, lanes(t)] = val
                half = (t * LANES) % W
                panel[t * LANES // W, pl.ds(pl.multiple_of(row_at * rows + i * RB, RB), RB), half:half + LANES] = val.astype(BF16)
            return 0
        lax.fori_loop(0, blocks, body, 0)

    def sinkhorn(r):
        low = row_exchange(cost_min(), 2, jnp.minimum)
        first = gibbs(low, 1.0 / eps_ref[r])
        u = p_ref[...] / row_exchange(first, 0, jnp.add)
        col_update(u, 0)

        def sweep(s, u):
            slot = s % 2
            u = p_ref[...] / row_exchange(row_sums(), slot, jnp.add)
            col_update(u, slot)
            return u
        u = lax.fori_loop(1, SWEEPS, sweep, u)
        make_plan(u)

    def stage_copy(i):
        return pltpu.make_async_copy(t_out.at[pl.ds(pl.multiple_of(i * SUB, SUB), SUB)], stage.at[i % 2], st_sem.at[i % 2])

    def loss():
        groups = rows // SUB
        stage_copy(0).start()

        def body(g, total):
            @pl.when(g + 1 < groups)
            def _():
                stage_copy(g + 1).start()
            stage_copy(g).wait()
            at = pl.ds(pl.multiple_of(g * SUB, SUB), SUB)
            a_rep = jnp.broadcast_to(unpack(a_ref[...], g), (SUB, LANES))
            part = None
            for t in range(tiles):
                val = ((a_rep + b_ref[:, lanes(t)]) - 2.0 * acc[at, lanes(t)]) * stage[g % 2, :, lanes(t)]
                part = val if part is None else part + val
            return total + part
        loss_out[...] = lax.fori_loop(0, groups, body, jnp.zeros((SUB, LANES), F32))

    first_plan = pltpu.make_async_copy(t0_ref, panel.at[:, rows_of(row_at)], io_sem)
    first_plan.start()
    first_plan.wait()
    plan_out = pltpu.make_async_copy(acc, t_out, io_sem)

    def outer(r, _):
        cost()

        @pl.when(r < steps)
        def _():
            sinkhorn(r)

        @pl.when(r == steps - 1)
        def _():
            plan_out.start()
            plan_out.wait()
        return 0
    lax.fori_loop(0, steps + 1, outer, 0)
    loss()


def packed_rows(vec):
    groups = vec.shape[0] // SUB
    return jnp.pad(vec.reshape(groups, SUB).T, ((0, 0), (0, LANES - groups)), constant_values=1.0)


def solution(mesh):
    grid_spec = P(("pairs", "rows"), "cols")

    def local_fn(c1_blk, c2_blk, t0_blk, p_blk, q_blk, eps_blk):
        col_pos = lax.axis_index("cols")
        row_pos = lax.axis_index("rows")
        c1_width = c1_blk.shape[1]
        c2_height = c2_blk.shape[0]
        rows, cols = t0_blk.shape
        chunks = cols // W
        steps = eps_blk.shape[0]
        p_full = lax.all_gather(p_blk, "rows", tiled=True)
        q_full = lax.all_gather(q_blk, "cols", tiled=True)
        p_piece = lax.dynamic_slice_in_dim(p_full, col_pos * c1_width, c1_width)
        q_piece = lax.dynamic_slice_in_dim(q_full, row_pos * c2_height, c2_height)
        row_term = lax.psum(jnp.sum(c1_blk * c1_blk * p_piece[None, :], axis=1), "cols")
        col_term = lax.psum(jnp.sum(c2_blk * c2_blk * q_piece[:, None], axis=0), "rows")
        c1_panel = lax.all_gather(c1_blk.astype(BF16), "cols", axis=1, tiled=True)
        c2_panel = lax.all_gather(c2_blk.astype(BF16), "rows", axis=0, tiled=True)
        t0_chunks = t0_blk.astype(BF16).reshape(rows, chunks, W).transpose(1, 0, 2)

        vmem = pl.BlockSpec(memory_space=pltpu.VMEM)
        smem = pl.BlockSpec(memory_space=pltpu.SMEM)
        hbm = pl.BlockSpec(memory_space=pl.ANY)
        dma = pltpu.SemaphoreType.DMA
        plan, loss_part = pl.pallas_call(
            functools.partial(outer_kernel, steps),
            out_shape=(jax.ShapeDtypeStruct((rows, cols), F32), jax.ShapeDtypeStruct((SUB, LANES), F32)),
            in_specs=[vmem, hbm, hbm, vmem, vmem, vmem, vmem, smem],
            out_specs=(hbm, vmem),
            scratch_shapes=[
                pltpu.VMEM((rows, cols), F32),
                pltpu.VMEM((chunks, 4 * rows, W), BF16),
                pltpu.VMEM((LEADS, rows, W), BF16),
                pltpu.VMEM((chunks, rows, W), BF16),
                pltpu.VMEM((2, W, cols), BF16),
                pltpu.VMEM((2, W, cols), BF16),
                pltpu.VMEM((1, cols), F32),
                pltpu.VMEM((3, SUB, LANES), F32),
                pltpu.VMEM((3, SUB, LANES), F32),
                pltpu.VMEM((2, 1, cols), F32),
                pltpu.VMEM((2, 3, 1, cols), F32),
                pltpu.VMEM((2, SUB, cols), F32),
                *[dma((chunks,))] * 8,
                dma((2,)), dma((2,)), dma((3,)), dma((3,)), dma((2, 3)), dma((2, 3)),
                dma, dma((2,)),
            ],
            compiler_params=pltpu.CompilerParams(collective_id=0, has_side_effects=True, vmem_limit_bytes=67043328),
        )(c1_panel, t0_chunks, c2_panel, packed_rows(row_term), col_term[None], packed_rows(p_blk), q_blk[None], eps_blk)
        return plan, lax.psum(jnp.sum(loss_part), ("rows", "cols")).reshape(1)

    return jax.shard_map(local_fn, mesh=mesh, in_specs=(grid_spec, grid_spec, grid_spec, P(("pairs", "rows")), P(("pairs", "cols")), P("pairs")), out_specs=(grid_spec, P("pairs")), check_vma=False)
```

time: 6440 us -> 2820 us (0.44)
  waiting for transfers between devices: 3130 us -> 382 us
  Pallas kernels: 0 us -> 2300 us
  blocking collectives: 1300 us -> 52.5 us
  other arithmetic: 1180 us -> 36.3 us
  matrix products: 792 us -> 0 us
    all_gather x20 -> x2, waiting for transfers between devices: 3130 us -> 382 us  [the longest x1 382 us: local_fn(): c2_panel = lax.all_gather(c2_blk.astype(BF16), 'rows', axis=0, tiled=True)]
    pallas_call x0 -> x1, Pallas kernels: none -> 2300 us  [local_fn(): pl.pallas_call(functools.partial(outer_kernel, steps), out_shape=(jax.Sha...]
    psum x161 -> x1, blocking collectives: 1230 us -> 22.4 us  [local_fn(): return (plan, lax.psum(jnp.sum(loss_part), ('rows', 'cols')).reshape(1))]
    reduce_sum x160 -> x1, other arithmetic: 943 us -> 1.28 us  [local_fn(): return (plan, lax.psum(jnp.sum(loss_part), ('rows', 'cols')).reshape(1))]
    dot_general x18 -> x0, matrix products: 792 us -> none  [the longest x9 560 us: cost_of(): jnp.dot(lead_panel, c2_panel, preferred_element_type=jnp.float32)]
    convert_element_type x9 -> x0, other arithmetic: 102 us -> none  [cost_of(): plan_blk.astype(jnp.bfloat16)]
    exp x8 -> x0, other arithmetic: 98.8 us -> none  [local_fn(): kernel = jnp.exp(-(cost_blk - row_shift[:, None]) / eps_blk[step_idx])]
  transfers between devices with their start and end apart: 20 -> 2, of which waited for: 20 -> 1; matrix products, arithmetic and copies ran while one was open for 1% -> 2% of each run, Pallas kernels for 0% -> 0%
where the time goes in v1:
time: 2820 us
  Pallas kernels  2300 us (82%)
  waiting for transfers between devices  382 us (14%)
  blocking collectives  52.5 us (2%)
  other arithmetic  36.3 us (1%)
  local copies, waits for them, and re-layouts  32.4 us (1%)
    pallas_call x1, Pallas kernels, local_fn(): pl.pallas_call(functools.partial(outer_kernel, steps), out_shape=(jax.Sha...  2300 us
    all_gather x1, waiting for transfers between devices, local_fn(): c2_panel = lax.all_gather(c2_blk.astype(BF16), 'rows', axis=0, tiled=True)  382 us
  transfers between devices with their start and end apart: 2, of which 1 were waited for; matrix products, arithmetic and copies ran while one was open for 2% of the time, Pallas kernels for 0%

profile of v1, /device:TPU:0, one launch (start us, length us, event | category | flops | bytes accessed | tf_op | source)
XLA Modules:
  0.0 2817.2 jit_solution(9656791278504632591)
XLA Ops:
  7.2 0.0 all-gather.4.cloned.1.call-start
  7.2 0.7 reshape.22
  7.9 10.0 all-gather
  17.9 0.1 dynamic_slice.6
  18.0 6.0 multiply_reduce_fusion.1
  24.0 0.0 all-gather.6.cloned.1.call-start
  24.1 4.4 all_gather.15
  28.5 29.0 %multiply_reduce_fusion = (f32[4096]{0:T(1024)S(1)}, bf16[2048,4096]{1,0:T(8,128)(2,1)}) fusion(f32[2048,4096]{1,0:T(8,128)} %param.7, f32[2048]{0:T(1024)S(1)} %dynamic_slice.7), kind=kLoop, calls=%fused_computation | loop fusion | flops 33550336 | bytes 50356224 | tf_op jit(solution)/shard_map/reduce_sum | solution.py:331
  57.5 0.7 copy-done
  58.2 0.1 reshape.20
  58.3 0.1 reshape.19
  58.4 0.1 copy.14
  58.4 10.0 copy.12
  68.4 8.7 copy.13
  77.0 0.1 copy.15
  77.1 5.0 psum.21
  82.1 0.6 pad.7.a_ref
  82.7 0.6 pad.8.p_ref
  83.3 10.7 psum.22.b_ref
  94.0 381.7 %all-gather.6.cloned.1.call-done.c2_ref = bf16[8192,4096]{1,0:T(8,128)(2,1)} async-done(((bf16[2048,4096]{1,0:T(8,128)(2,1)}), bf16[8192,4096]{1,0:T(8,128)(2,1)}) %all-gather.6.cloned.1.call-update) | async-done | bytes 67108880 | tf_op jit(solution)/shard_map/all_gather | solution.py:333
  475.7 2300.0 %shard_map.77 = (f32[768,4096]{1,0:T(8,128)}, f32[8,128]{1,0:T(8,128)}) custom-call(bf16[768,3072]{1,0:T(8,128)(2,1)} %all-gather.4.cloned.1.call-done.c1_ref, bf16[16,768,256]{2,1,0:T(8,128)(2,1)} %bitcast.8, bf16[8192,4096]{1,0:T(8,128)(2,1)} %all-gather.6.cloned.1.call-done.c2_ref, f32[8,128]{1,0:T(8,128)} %pad.7.a_ref, f32[1,4096]{1,0:T(1,128)} %psum.22.b_ref, ...), custom_call_target="tpu_custom_call" | custom-call | tf_op jit(solution)/shard_map/pallas_call | solution.py:340
  2775.7 1.3 reduce_sum.29
  2777.0 22.4 psum.23
  2799.4 10.9 copy.17
  (5 shorter events, 0.0 us)
Async XLA Ops:
  7.2 86.8 %all-gather.4.cloned.1.call-start = ((), (), s32[]{:S(2)}) async-start(), calls=%async_computation | async-start | bytes 7077888 | tf_op jit(solution)/shard_map/all_gather | solution.py:332
  24.0 451.7 %all-gather.6.cloned.1.call-start = ((), (), s32[]{:S(2)}) async-start(), calls=%async_computation.1 | async-start | bytes 83886080 | tf_op jit(solution)/shard_map/all_gather | solution.py:333
  57.5 0.7 copy-start
Sparse Core Ops, SparseCore 0:
  24.1 60.3 all-gather.3
  86.0 389.6 all-gather.5

commit v2 on v1

v2 whole, which is shorter than its diff:
```python
import functools

import jax
import jax.numpy as jnp
from jax import lax
from jax.experimental import pallas as pl
from jax.experimental.pallas import tpu as pltpu
from jax.sharding import PartitionSpec as P

SWEEPS = 10
W = 256
AHEAD = 4
RB = 64
HALF = 8
LANES = 128
SUB = 8
F32 = jnp.float32
BF16 = jnp.bfloat16


def outer_kernel(steps, c1_blk, t0_ref, c2_blk, a_ref, b_part, p_ref, q_ref, eps_ref, t_out, loss_out, c2_ref, c2_turn,
                 acc, panel, c1_ref, lead_in, c2_own, c2_in, turn_in, turn_out, b_ref, v_ref, a_rep, u_rep, part, c_part,
                 m_send, m_in, r_send, r_in, c_send, c_in, stage,
                 x_send, x_recv, d_send, d_recv, f_send, f_recv, y_send, y_recv,
                 own_sem, in_sem, ms_sem, mr_sem, rs_sem, rr_sem, cs_sem, cr_sem, io_sem, st_sem,
                 xs_sem, xr_sem, ts_sem, tr_sem, fs_sem, fr_sem, us_sem, ur_sem, bs_sem, br_sem, os_sem, or_sem, turn_sem):
    rows, cols = acc.shape
    chunks = cols // W
    row_at = lax.axis_index("rows")
    col_at = lax.axis_index("cols")
    chip, core = row_at // 2, row_at % 2
    sib = chip * 2 + (1 - core)
    across = (1 - chip) * 2 + core
    diag = (1 - chip) * 2 + (1 - core)
    to_sib, to_across, to_diag, to_col = {"rows": sib}, {"rows": across}, {"rows": diag}, {"cols": 1 - col_at}
    trio = (to_sib, to_across, to_diag)

    barrier = pltpu.get_barrier_semaphore()
    for dev in (*trio, to_col):
        pl.semaphore_signal(barrier, inc=1, device_id=dev)
    pl.semaphore_wait(barrier, 4)

    def rows_of(owner):
        return pl.ds(pl.multiple_of(owner * rows, rows), rows)

    def lead_at(j):
        return panel.at[j, rows_of(sib)]

    def x_copy(j):
        part = panel.at[j, rows_of(row_at)]
        return pltpu.make_async_remote_copy(part, part, x_send.at[j], x_recv.at[j], device_id=to_across)

    def d_copy(j):
        part = panel.at[j, rows_of(row_at)]
        return pltpu.make_async_remote_copy(part, part, d_send.at[j], d_recv.at[j], device_id=to_sib)

    def f_copy(j):
        part = panel.at[j, rows_of(across)]
        return pltpu.make_async_remote_copy(part, part, f_send.at[j], f_recv.at[j], device_id=to_sib)

    def y_copy(j):
        return pltpu.make_async_remote_copy(lead_at(j), lead_in.at[j], y_send.at[j], y_recv.at[j], device_id=to_col)

    held = c2_blk.shape[0]
    here = held // W

    def wide(n):
        return pl.ds(pl.multiple_of(n * W, W), W)

    def c2_start(owner, i, buf, sem):
        block = owner * (chunks // here) + i // here

        @pl.when(block == row_at)
        def _():
            pltpu.make_async_copy(c2_blk.at[wide(i % here)], buf.at[i % 2], sem.at[i % 2]).start()

        @pl.when(block != row_at)
        def _():
            for n in range(chunks):
                pltpu.make_async_copy(c2_ref.at[n, wide(owner * chunks + i)], buf.at[i % 2, :, n * W:(n + 1) * W], sem.at[i % 2]).start()

    def c2_wait(i, buf, sem):
        pltpu.make_async_copy(c2_blk.at[0:W], buf.at[i % 2], sem.at[i % 2]).wait()

    def add_product(left, right, first):
        tile = 512

        def body(n, _):
            at = pl.ds(pl.multiple_of(n * tile, tile), tile)
            prod = jnp.dot(left[...], right[:, at], preferred_element_type=F32)
            if first:
                acc[:, at] = prod
            else:
                acc[:, at] = acc[:, at] + prod
            return 0
        lax.fori_loop(0, cols // tile, body, 0)

    lane = lax.broadcasted_iota(jnp.int32, (SUB, LANES), 1)

    def lanes(t):
        return slice(t * LANES, (t + 1) * LANES)

    tiles = cols // LANES
    per = RB // SUB
    blocks = rows // RB
    groups = rows // SUB

    def issue(j):
        x_copy(j).start()
        d_copy(j).start()

    def product(owner, i, left, buf, sem, first=False):
        c2_wait(i, buf, sem)
        add_product(left, buf.at[i % 2], first)

        @pl.when(i + 2 < chunks)
        def _():
            c2_start(owner, i + 2, buf, sem)

    def take_chunk(j):
        x_copy(j).wait_recv()
        f_copy(j).start()

        @pl.when(j + AHEAD < chunks)
        def _():
            issue(j + AHEAD)

    def form_lead(j):
        d_copy(j).wait_recv()
        f_copy(j).wait_recv()
        panel[j, rows_of(sib)] = jnp.dot(c1_ref[...], panel[j], preferred_element_type=F32).astype(BF16)
        y_copy(j).start()

    def drain_chunks():
        def drain(j, _):
            x_copy(j).wait_send()
            d_copy(j).wait_send()
            f_copy(j).wait_send()
            y_copy(j).wait_send()
            return 0
        lax.fori_loop(0, chunks, drain, 0)

    def cost():
        for i in range(2):
            c2_start(col_at, i, c2_own, own_sem)
            c2_start(1 - col_at, i, c2_in, in_sem)

        def step(j, _):
            @pl.when(j < chunks)
            def _():
                take_chunk(j)

            @pl.when(j == 1)
            def _():
                product(col_at, 0, lead_at(0), c2_own, own_sem, True)

            @pl.when((j > 1) & (j <= chunks))
            def _():
                product(col_at, j - 1, lead_at(j - 1), c2_own, own_sem)

            @pl.when(j < chunks)
            def _():
                form_lead(j)

            @pl.when(j >= 2)
            def _():
                y_copy(j - 2).wait_recv()
                product(1 - col_at, j - 2, lead_in.at[j - 2], c2_in, in_sem)
            return 0
        lax.fori_loop(0, chunks + 2, step, 0)
        drain_chunks()

    far = 1 - chip

    def quad_rows(base, k):
        return pl.ds(pl.multiple_of(base + k * W, W), W)

    def many(ref, count):
        return ref.at[pl.ds(0, count), pl.ds(0, W)]

    def own_piece(n, m):
        return c2_blk.at[wide(m), wide(n)]

    def sends(src, dst, dst_base, k, m, offsets, sem_s, sem_r, dev):
        for d in offsets:
            n = (k + d) % chunks
            to = dst.at[n, quad_rows(dst_base, m)]
            pltpu.make_async_remote_copy(own_piece(n, m) if src is None else src.at[n, quad_rows(dst_base, m)], to,
                                         sem_s.at[m], sem_r.at[m], device_id=dev).start()

    def group(m, count, sem_s, sem_r, dev):
        return pltpu.make_async_remote_copy(many(c2_ref, count), many(c2_ref, count), sem_s.at[m], sem_r.at[m], device_id=dev)

    straight, turned = range(HALF + 1), range(1, HALF)
    across_base, turn_base = across * held, core * held

    def row_send(m):
        k = core * here + m
        sends(None, c2_ref, row_at * held, k, m, straight, xs_sem, xr_sem, to_across)
        sends(None, c2_turn, turn_base, k, m, turned, ts_sem, tr_sem, to_col)

    def row_forward(m):
        k = core * here + m
        group(m, HALF + 1, xs_sem, xr_sem, to_across).wait_recv()
        sends(c2_ref, c2_ref, across_base, k, m, straight, fs_sem, fr_sem, to_sib)
        group(m, HALF - 1, ts_sem, tr_sem, to_col).wait_recv()
        sends(c2_turn, c2_turn, turn_base, k, m, turned, us_sem, ur_sem, to_sib)

    def row_turn(k):
        def load(src, base):
            for d in turned:
                pltpu.make_async_copy(src.at[(k + d) % chunks, quad_rows(base, k)], turn_in.at[d - 1], turn_sem.at[0]).start()

        @pl.when(chip == col_at)
        def _():
            load(c2_turn, 0)

        @pl.when(chip != col_at)
        def _():
            load(c2_ref, far * cols)
        pltpu.make_async_copy(many(c2_ref, HALF - 1), turn_in, turn_sem.at[0]).wait()
        for d in turned:
            turn_out[d - 1] = turn_in[d - 1].T
        for d in turned:
            pltpu.make_async_copy(turn_out.at[d - 1], c2_ref.at[k, quad_rows(far * cols, (k + d) % chunks)], turn_sem.at[1]).start()
        pltpu.make_async_copy(turn_out, many(c2_ref, HALF - 1), turn_sem.at[1]).wait()

    def first_cost(own_block, c1_copy):
        own_block.wait_recv()
        for i in range(2):
            c2_start(chip, i, c2_own, own_sem)

        def step(j, _):
            @pl.when((j < chunks) & (j % 2 == 0))
            def _():
                row_send(j // 2)

            @pl.when(j < chunks)
            def _():
                take_chunk(j)

            @pl.when((j == 1) & (chip == col_at))
            def _():
                product(chip, 0, lead_at(0), c2_own, own_sem, True)

            @pl.when((j > 1) & (j <= chunks) & (chip == col_at))
            def _():
                product(chip, j - 1, lead_at(j - 1), c2_own, own_sem)

            @pl.when(j == 0)
            def _():
                c1_copy.wait_recv()

            @pl.when(j < chunks)
            def _():
                form_lead(j)

            @pl.when(j >= 2)
            def _():
                y_copy(j - 2).wait_recv()

            @pl.when((j == 2) & (chip != col_at))
            def _():
                product(chip, 0, lead_in.at[0], c2_own, own_sem, True)

            @pl.when((j > 2) & (chip != col_at))
            def _():
                product(chip, j - 2, lead_in.at[j - 2], c2_own, own_sem)

            @pl.when((j > 2) & (j % 2 == 1))
            def _():
                m = (j - 3) // 2
                row_forward(m)
                row_turn(core * here + m)
                group(m, HALF + 1, fs_sem, fr_sem, to_sib).wait_recv()
                group(m, HALF - 1, us_sem, ur_sem, to_sib).wait_recv()
                row_turn((1 - core) * here + m)
            return 0
        lax.fori_loop(0, chunks + 2, step, 0)

        for i in range(2):
            c2_start(far, i, c2_in, in_sem)

        def rest(i, _):
            @pl.when(chip == col_at)
            def _():
                product(far, i, lead_in.at[i], c2_in, in_sem)

            @pl.when(chip != col_at)
            def _():
                product(far, i, lead_at(i), c2_in, in_sem)
            return 0
        lax.fori_loop(0, chunks, rest, 0)
        drain_chunks()
        own_block.wait_send()
        c1_copy.wait_send()

        def sent_rows(m, _):
            group(m, HALF + 1, xs_sem, xr_sem, to_across).wait_send()
            group(m, HALF - 1, ts_sem, tr_sem, to_col).wait_send()
            group(m, HALF + 1, fs_sem, fr_sem, to_sib).wait_send()
            group(m, HALF - 1, us_sem, ur_sem, to_sib).wait_send()
            return 0
        lax.fori_loop(0, here, sent_rows, 0)

    def spread(packed, out, groups):
        for g in groups:
            val = jnp.sum(jnp.where(lane == g, packed, 0.0), axis=1, keepdims=True)
            out[g * SUB:(g + 1) * SUB] = jnp.broadcast_to(val, (SUB, LANES))

    def gather_rows(reduce, groups):
        packed = jnp.ones((SUB, LANES), F32)
        for g in groups:
            packed = jnp.where(lane == g, reduce(part[g * SUB:(g + 1) * SUB], axis=1, keepdims=True), packed)
        return packed

    def block_at(i):
        return pl.ds(pl.multiple_of(i * RB, RB), RB)

    def cost_min():
        def body(i, _):
            at = block_at(i)
            a_rows = a_rep[at]
            low = None
            for t in range(tiles):
                val = (a_rows + b_ref[:, lanes(t)]) - 2.0 * acc[at, lanes(t)]
                acc[at, lanes(t)] = val
                low = val if low is None else jnp.minimum(low, val)
            part[at] = low
            return 0
        lax.fori_loop(0, blocks, body, 0)
        m_send[...] = gather_rows(jnp.min, range(groups))
        copy = pltpu.make_async_remote_copy(m_send, m_in, ms_sem, mr_sem, device_id=to_col)
        copy.start()
        copy.wait()
        spread(jnp.minimum(m_send[...], m_in[...]), u_rep, range(groups))

    def gibbs(scale):
        def body(i, _):
            at = block_at(i)
            low = u_rep[at]
            total = None
            for t in range(tiles):
                val = jnp.exp((low - acc[at, lanes(t)]) * scale)
                acc[at, lanes(t)] = val
                total = val if total is None else total + val
            part[at] = total
            return 0
        lax.fori_loop(0, blocks, body, 0)

    def row_pass(first_block, last_block, half):
        def body(i, _):
            at = block_at(i)
            total = part[at] if half else None
            for t in range(half * tiles // 2, (half + 1) * tiles // 2):
                val = acc[at, lanes(t)] * v_ref[:, lanes(t)]
                total = val if total is None else total + val
            part[at] = total
            return 0
        lax.fori_loop(first_block, last_block, body, 0)

    def col_pass(first_block, last_block, half, first):
        mine = range(half * tiles // 2, (half + 1) * tiles // 2)

        def body(i, sums):
            reps = [u_rep[pl.ds(pl.multiple_of(i * RB + k * SUB, SUB), SUB)] for k in range(per)]
            out = []
            for t, val in zip(mine, sums):
                for k in range(per):
                    val = val + acc[pl.ds(pl.multiple_of(i * RB + k * SUB, SUB), SUB), lanes(t)] * reps[k]
                out.append(val)
            return tuple(out)
        start = tuple(jnp.zeros((SUB, LANES), F32) if first else c_part[:, lanes(t)] for t in mine)
        return lax.fori_loop(first_block, last_block, body, start)

    def r_copy(slot, half):
        return pltpu.make_async_remote_copy(r_send.at[slot, half], r_in.at[slot, half], rs_sem.at[slot, half], rr_sem.at[slot, half], device_id=to_col)

    def c_copies(slot, half):
        return [
            pltpu.make_async_remote_copy(c_send.at[slot, half], c_in.at[slot, half, n], cs_sem.at[slot, half, n], cr_sem.at[slot, half, n], device_id=dev)
            for n, dev in enumerate(trio)
        ]

    mid_group, mid_block, mid_col = groups // 2, blocks // 2, cols // 2

    def send_rows(slot, half):
        r_send[slot, half] = gather_rows(jnp.sum, range(half * mid_group, (half + 1) * mid_group))
        r_copy(slot, half).start()

    def take_rows(slot, half):
        r_copy(slot, half).wait_recv()
        u = p_ref[...] / (r_send[slot, half] + r_in[slot, half])
        spread(u, u_rep, range(half * mid_group, (half + 1) * mid_group))

    def send_cols(slot, half, sums):
        for t, val in enumerate(sums):
            c_send[slot, half, :, lanes(t)] = jnp.sum(val, axis=0, keepdims=True)
        for copy in c_copies(slot, half):
            copy.start()

    def take_cols(slot, half):
        for copy in c_copies(slot, half):
            copy.wait_recv()
        at = slice(half * mid_col, (half + 1) * mid_col)
        total = (c_send[slot, half] + c_in[slot, half, 0]) + (c_in[slot, half, 1] + c_in[slot, half, 2])
        v_ref[:, at] = q_ref[:, at] / total

    def sent(slot):
        for half in range(2):
            r_copy(slot, half).wait_send()
            for copy in c_copies(slot, half):
                copy.wait_send()

    def make_plan():
        def chunk(j, _):
            def body(i, _):
                at = block_at(i)
                for t in range(W // LANES):
                    where = pl.ds(pl.multiple_of(j * W + t * LANES, LANES), LANES)
                    val = (u_rep[at] * acc[at, where]) * v_ref[:, where]
                    acc[at, where] = val
                    panel[j, pl.ds(pl.multiple_of(row_at * rows + i * RB, RB), RB), lanes(t)] = val.astype(BF16)
                return 0
            lax.fori_loop(0, blocks, body, 0)

            @pl.when(j < AHEAD)
            def _():
                issue(j)
            return 0
        lax.fori_loop(0, chunks, chunk, 0)

    def sinkhorn(r):
        cost_min()
        gibbs(1.0 / eps_ref[r])

        def sweep(s, _):
            slot = s % 2

            @pl.when(s == 0)
            def _():
                send_rows(slot, 0)
                send_rows(slot, 1)

            @pl.when(s > 0)
            def _():
                take_cols(1 - slot, 0)
                row_pass(0, blocks, 0)
                take_cols(1 - slot, 1)
                row_pass(0, mid_block, 1)
                send_rows(slot, 0)
                row_pass(mid_block, blocks, 1)
                send_rows(slot, 1)

            take_rows(slot, 0)
            for half in range(2):
                for t, val in enumerate(col_pass(0, mid_block, half, True)):
                    c_part[:, lanes(half * tiles // 2 + t)] = val
            take_rows(slot, 1)
            for half in range(2):
                send_cols(slot, half, col_pass(mid_block, blocks, half, False))

            @pl.when(s > 0)
            def _():
                sent(1 - slot)
            return 0
        lax.fori_loop(0, SWEEPS, sweep, 0)
        last = (SWEEPS - 1) % 2
        for half in range(2):
            take_cols(last, half)
        sent(last)
        make_plan()

    def stage_copy(i):
        return pltpu.make_async_copy(t_out.at[pl.ds(pl.multiple_of(i * SUB, SUB), SUB)], stage.at[i % 2], st_sem.at[i % 2])

    def loss():
        stage_copy(0).start()

        def body(g, total):
            @pl.when(g + 1 < groups)
            def _():
                stage_copy(g + 1).start()
            stage_copy(g).wait()
            at = pl.ds(pl.multiple_of(g * SUB, SUB), SUB)
            a_rows = a_rep[at]
            out = None
            for t in range(tiles):
                val = ((a_rows + b_ref[:, lanes(t)]) - 2.0 * acc[at, lanes(t)]) * stage[g % 2, :, lanes(t)]
                out = val if out is None else out + val
            return total + out
        loss_out[...] = lax.fori_loop(0, groups, body, jnp.zeros((SUB, LANES), F32))

    for j in range(chunks):
        pltpu.make_async_copy(t0_ref.at[:, j * W:(j + 1) * W], panel.at[j, rows_of(row_at)], io_sem).start()
    first_plan = pltpu.make_async_copy(panel.at[:, rows_of(row_at)], panel.at[:, rows_of(row_at)], io_sem)
    width = c1_blk.shape[1]
    c1_at = c1_ref.at[:, pl.ds(pl.multiple_of(col_at * width, width), width)]
    c1_here = pltpu.make_async_copy(c1_blk, c1_at, st_sem.at[0])
    c1_here.start()
    c1_copy = pltpu.make_async_remote_copy(c1_blk, c1_at, os_sem, or_sem, device_id=to_col)
    c1_copy.start()
    own_rows = c2_ref.at[:, pl.ds(pl.multiple_of(row_at * held, held), held)]
    own_block = pltpu.make_async_remote_copy(own_rows, own_rows, bs_sem, br_sem, device_id=to_sib)
    for n in range(chunks):
        piece = c2_blk.at[:, n * W:(n + 1) * W]
        pltpu.make_async_remote_copy(piece, own_rows.at[n], bs_sem, br_sem, device_id=to_sib).start()
    first_plan.wait()
    for j in range(AHEAD):
        issue(j)

    m_send[...] = a_ref[...]
    a_copy = pltpu.make_async_remote_copy(m_send, m_in, ms_sem, mr_sem, device_id=to_col)
    a_copy.start()
    for half in range(2):
        c_send[0, half] = b_part[:, half * mid_col:(half + 1) * mid_col]
        for copy in c_copies(0, half):
            copy.start()
    a_copy.wait()
    spread(m_send[...] + m_in[...], a_rep, range(groups))
    for half in range(2):
        for copy in c_copies(0, half):
            copy.wait()
        total = (c_send[0, half] + c_in[0, half, 0]) + (c_in[0, half, 1] + c_in[0, half, 2])
        b_ref[:, half * mid_col:(half + 1) * mid_col] = total
    c1_here.wait()
    plan_out = pltpu.make_async_copy(acc, t_out, io_sem)
    first_cost(own_block, c1_copy)

    def outer(r, _):
        sinkhorn(r)

        @pl.when(r == steps - 1)
        def _():
            plan_out.start()
            plan_out.wait()
        cost()
        return 0
    lax.fori_loop(0, steps, outer, 0)
    loss()


def packed_rows(vec):
    groups = vec.shape[0] // SUB
    return jnp.pad(vec.reshape(groups, SUB).T, ((0, 0), (0, LANES - groups)), constant_values=1.0)


def solution(mesh):
    grid_spec = P(("pairs", "rows"), "cols")

    def local_fn(c1_blk, c2_blk, t0_blk, p_blk, q_blk, eps_blk):
        col_pos = lax.axis_index("cols")
        row_pos = lax.axis_index("rows")
        c1_width = c1_blk.shape[1]
        c2_height = c2_blk.shape[0]
        rows, cols = t0_blk.shape
        chunks = cols // W
        steps = eps_blk.shape[0]
        p_full = lax.all_gather(p_blk, "rows", tiled=True)
        q_full = lax.all_gather(q_blk, "cols", tiled=True)
        p_piece = lax.dynamic_slice_in_dim(p_full, col_pos * c1_width, c1_width)
        q_piece = lax.dynamic_slice_in_dim(q_full, row_pos * c2_height, c2_height)
        row_term = jnp.sum(c1_blk * c1_blk * p_piece[None, :], axis=1)
        col_term = jnp.sum(c2_blk * c2_blk * q_piece[:, None], axis=0)

        vmem = pl.BlockSpec(memory_space=pltpu.VMEM)
        smem = pl.BlockSpec(memory_space=pltpu.SMEM)
        hbm = pl.BlockSpec(memory_space=pl.ANY)
        dma = pltpu.SemaphoreType.DMA
        plan, loss_part, _, _ = pl.pallas_call(
            functools.partial(outer_kernel, steps),
            out_shape=(
                jax.ShapeDtypeStruct((rows, cols), F32), jax.ShapeDtypeStruct((SUB, LANES), F32),
                jax.ShapeDtypeStruct((chunks, 2 * cols, W), BF16), jax.ShapeDtypeStruct((chunks, cols, W), BF16),
            ),
            in_specs=[hbm, hbm, hbm, vmem, vmem, vmem, vmem, smem],
            out_specs=(hbm, vmem, hbm, hbm),
            scratch_shapes=[
                pltpu.VMEM((rows, cols), F32),
                pltpu.VMEM((chunks, 4 * rows, W), BF16),
                pltpu.VMEM((rows, 4 * rows), BF16),
                pltpu.VMEM((chunks, rows, W), BF16),
                pltpu.VMEM((2, W, cols), BF16),
                pltpu.VMEM((2, W, cols), BF16),
                pltpu.VMEM((HALF - 1, W, W), BF16),
                pltpu.VMEM((HALF - 1, W, W), BF16),
                pltpu.VMEM((1, cols), F32),
                pltpu.VMEM((1, cols), F32),
                *[pltpu.VMEM((rows, LANES), F32)] * 3,
                pltpu.VMEM((SUB, cols), F32),
                pltpu.VMEM((SUB, LANES), F32),
                pltpu.VMEM((SUB, LANES), F32),
                pltpu.VMEM((2, 2, SUB, LANES), F32),
                pltpu.VMEM((2, 2, SUB, LANES), F32),
                pltpu.VMEM((2, 2, 1, cols // 2), F32),
                pltpu.VMEM((2, 2, 3, 1, cols // 2), F32),
                pltpu.VMEM((2, SUB, cols), F32),
                *[dma((chunks,))] * 8,
                dma((2,)), dma((2,)), dma, dma, dma((2, 2)), dma((2, 2)), dma((2, 2, 3)), dma((2, 2, 3)),
                dma, dma((2,)),
                *[dma((c2_height // W,))] * 8,
                dma, dma, dma, dma, dma((2,)),
            ],
            compiler_params=pltpu.CompilerParams(collective_id=0, has_side_effects=True, vmem_limit_bytes=67043328),
        )(c1_blk.astype(BF16), t0_blk.astype(BF16), c2_blk.astype(BF16), packed_rows(row_term), col_term[None], packed_rows(p_blk), q_blk[None], eps_blk)
        return plan, lax.psum(jnp.sum(loss_part), ("rows", "cols")).reshape(1)

    return jax.shard_map(local_fn, mesh=mesh, in_specs=(grid_spec, grid_spec, grid_spec, P(("pairs", "rows")), P(("pairs", "cols")), P("pairs")), out_specs=(grid_spec, P("pairs")), check_vma=False)
```

time: 2820 us -> 2430 us (0.86)
  waiting for transfers between devices: 382 us -> 0 us
  Pallas kernels: 2300 us -> 2330 us
    all_gather x2 -> x0, waiting for transfers between devices: 382 us -> none  [the longest x1 382 us: local_fn(): c2_panel = lax.all_gather(c2_blk.astype(BF16), 'rows', axis=0, tiled=True)]
    pallas_call x1, Pallas kernels: 2300 us -> 2330 us  [local_fn(): pl.pallas_call(functools.partial(outer_kernel, steps), out_shape=(jax.Sha...]
  transfers between devices with their start and end apart: 2 -> 0, of which waited for: 1 -> 0; matrix products, arithmetic and copies ran while one was open for 2% -> 0% of each run, Pallas kernels for 0% -> 0%
where the time goes in v2:
time: 2430 us
  Pallas kernels  2330 us (96%)
  other arithmetic  45.2 us (2%)
  blocking collectives  36.8 us (2%)
    pallas_call x1, Pallas kernels, local_fn(): pl.pallas_call(functools.partial(outer_kernel, steps), out_shape=(jax.Sha...  2330 us

profile of v2, /device:TPU:0, one launch (start us, length us, event | category | flops | bytes accessed | tf_op | source)
XLA Modules:
  0.0 2429.4 jit_solution(2309709845343138978)
XLA Ops:
  0.6 0.7 reshape.18
  1.3 10.0 all-gather
  11.3 0.1 dynamic_slice.6
  11.4 4.4 all_gather.7
  15.8 0.8 reshape.16
  16.5 0.1 copy.11
  16.6 0.6 pad.8.p_ref
  17.2 6.0 multiply_reduce_fusion.1
  23.2 0.1 reshape.15
  23.3 0.1 copy.10
  23.3 0.6 pad.7.a_ref
  24.0 8.2 convert_element_type.10.t0_ref
  32.2 29.7 %multiply_reduce_fusion = (f32[4096]{0:T(1024)}, bf16[2048,4096]{1,0:T(8,128)(2,1)}) fusion(f32[2048,4096]{1,0:T(8,128)} %param.7, f32[2048]{0:T(1024)S(1)} %dynamic_slice.7), kind=kLoop, calls=%fused_computation | loop fusion | flops 33550336 | bytes 50356224 | tf_op jit(solution)/shard_map/reduce_sum | solution.py:564
  61.9 2332.9 %shard_map.77 = (f32[768,4096]{1,0:T(8,128)}, f32[8,128]{1,0:T(8,128)}, bf16[16,8192,256]{2,1,0:T(8,128)(2,1)}, bf16[16,4096,256]{2,1,0:T(8,128)(2,1)}) custom-call(bf16[768,1536]{1,0:T(8,128)(2,1)} %get-tuple-element.9.c1_blk, bf16[768,4096]{1,0:T(8,128)(2,1)} %convert_element_type.10.t0_ref, bf16[2048,4096]{1,0:T(8,128)(2,1)} %get-tuple-element.7.c2_blk, ...), custom_call_target="tpu_custom_call" | custom-call | tf_op jit(solution)/shard_map/pallas_call | solution.py:570
  2394.7 1.3 reduce_sum.29
  2396.0 22.4 psum.7
  2418.5 10.9 copy.13
  (1 shorter events, 0.0 us)

commit v3 on v2

--- a/solution.py
+++ b/solution.py
@@ -19,7 +19,7 @@
 
 
 def outer_kernel(steps, c1_blk, t0_ref, c2_blk, a_ref, b_part, p_ref, q_ref, eps_ref, t_out, loss_out, c2_ref, c2_turn,
-                 acc, panel, c1_ref, lead_in, c2_own, c2_in, turn_in, turn_out, b_ref, v_ref, a_rep, u_rep, part, c_part,
+                 acc, panel, c1_ref, lead_in, c2_own, c2_in, turn_in, turn_out, b_ref, v_ref, a_rep, u_rep, part, c_part, f_ref,
                  m_send, m_in, r_send, r_in, c_send, c_in, stage,
                  x_send, x_recv, d_send, d_recv, f_send, f_recv, y_send, y_recv,
                  own_sem, in_sem, ms_sem, mr_sem, rs_sem, rr_sem, cs_sem, cr_sem, io_sem, st_sem,
@@ -46,20 +46,30 @@
     def lead_at(j):
         return panel.at[j, rows_of(sib)]
 
-    def x_copy(j):
-        part = panel.at[j, rows_of(row_at)]
-        return pltpu.make_async_remote_copy(part, part, x_send.at[j], x_recv.at[j], device_id=to_across)
-
-    def d_copy(j):
-        part = panel.at[j, rows_of(row_at)]
-        return pltpu.make_async_remote_copy(part, part, d_send.at[j], d_recv.at[j], device_id=to_sib)
-
-    def f_copy(j):
-        part = panel.at[j, rows_of(across)]
-        return pltpu.make_async_remote_copy(part, part, f_send.at[j], f_recv.at[j], device_id=to_sib)
-
-    def y_copy(j):
-        return pltpu.make_async_remote_copy(lead_at(j), lead_in.at[j], y_send.at[j], y_recv.at[j], device_id=to_col)
+    last = chunks - 1
+    halves = (0, 1)
+
+    def cut(owner, j, half):
+        if half is None:
+            return panel.at[j, rows_of(owner)], j
+        return panel.at[last, rows_of(owner), half * LANES:(half + 1) * LANES], last + half
+
+    def x_copy(j, half=None):
+        piece, n = cut(row_at, j, half)
+        return pltpu.make_async_remote_copy(piece, piece, x_send.at[n], x_recv.at[n], device_id=to_across)
+
+    def d_copy(j, half=None):
+        piece, n = cut(row_at, j, half)
+        return pltpu.make_async_remote_copy(piece, piece, d_send.at[n], d_recv.at[n], device_id=to_sib)
+
+    def f_copy(j, half=None):
+        piece, n = cut(across, j, half)
+        return pltpu.make_async_remote_copy(piece, piece, f_send.at[n], f_recv.at[n], device_id=to_sib)
+
+    def y_copy(j, half=None):
+        piece, n = cut(sib, j, half)
+        dst = lead_in.at[j] if half is None else lead_in.at[last, :, half * LANES:(half + 1) * LANES]
+        return pltpu.make_async_remote_copy(piece, dst, y_send.at[n], y_recv.at[n], device_id=to_col)
 
     held = c2_blk.shape[0]
     here = held // W
@@ -121,15 +131,32 @@
         x_copy(j).wait_recv()
         f_copy(j).start()
 
-        @pl.when(j + AHEAD < chunks)
+        @pl.when(j + AHEAD < last)
         def _():
             issue(j + AHEAD)
+
+        @pl.when(j + AHEAD == last)
+        def _():
+            for half in halves:
+                x_copy(last, half).start()
+                d_copy(last, half).start()
 
     def form_lead(j):
         d_copy(j).wait_recv()
         f_copy(j).wait_recv()
         panel[j, rows_of(sib)] = jnp.dot(c1_ref[...], panel[j], preferred_element_type=F32).astype(BF16)
         y_copy(j).start()
+
+    def last_chunk(between):
+        for half, meanwhile in zip(halves, between):
+            x_copy(last, half).wait_recv()
+            f_copy(last, half).start()
+            meanwhile()
+            d_copy(last, half).wait_recv()
+            f_copy(last, half).wait_recv()
+            cols_of = slice(half * LANES, (half + 1) * LANES)
+            panel[last, rows_of(sib), cols_of] = jnp.dot(c1_ref[...], panel[last, :, cols_of], preferred_element_type=F32).astype(BF16)
+            y_copy(last, half).start()
 
     def drain_chunks():
         def drain(j, _):
@@ -138,36 +165,55 @@
             f_copy(j).wait_send()
             y_copy(j).wait_send()
             return 0
-        lax.fori_loop(0, chunks, drain, 0)
+        lax.fori_loop(0, last, drain, 0)
+        for half in halves:
+            x_copy(last, half).wait_send()
+            d_copy(last, half).wait_send()
+            f_copy(last, half).wait_send()
+            y_copy(last, half).wait_send()
 
     def cost():
         for i in range(2):
             c2_start(col_at, i, c2_own, own_sem)
             c2_start(1 - col_at, i, c2_in, in_sem)
 
+        def own_part(i, first=False):
+            product(col_at, i, lead_at(i), c2_own, own_sem, first)
+
+        def in_part(i):
+            product(1 - col_at, i, lead_in.at[i], c2_in, in_sem)
+
         def step(j, _):
-            @pl.when(j < chunks)
-            def _():
-                take_chunk(j)
+            take_chunk(j)
 
             @pl.when(j == 1)
             def _():
-                product(col_at, 0, lead_at(0), c2_own, own_sem, True)
-
-            @pl.when((j > 1) & (j <= chunks))
-            def _():
-                product(col_at, j - 1, lead_at(j - 1), c2_own, own_sem)
-
-            @pl.when(j < chunks)
-            def _():
-                form_lead(j)
+                own_part(0, True)
+
+            @pl.when(j > 1)
+            def _():
+                own_part(j - 1)
+
+            form_lead(j)
 
             @pl.when(j >= 2)
             def _():
                 y_copy(j - 2).wait_recv()
-                product(1 - col_at, j - 2, lead_in.at[j - 2], c2_in, in_sem)
-            return 0
-        lax.fori_loop(0, chunks + 2, step, 0)
+                in_part(j - 2)
+            return 0
+        lax.fori_loop(0, last, step, 0)
+
+        def tail(i, _):
+            y_copy(i).wait_recv()
+            in_part(i)
+            return 0
+
+        last_chunk((lambda: own_part(last - 1), lambda: tail(last - 2, 0)))
+        own_part(last)
+        tail(last - 1, 0)
+        for half in halves:
+            y_copy(last, half).wait_recv()
+        in_part(last)
         drain_chunks()
 
     far = 1 - chip
@@ -235,7 +281,7 @@
             def _():
                 row_send(j // 2)
 
-            @pl.when(j < chunks)
+            @pl.when(j < last)
             def _():
                 take_chunk(j)
 
@@ -251,13 +297,22 @@
             def _():
                 c1_copy.wait_recv()
 
-            @pl.when(j < chunks)
+            @pl.when(j < last)
             def _():
                 form_lead(j)
 
-            @pl.when(j >= 2)
+            @pl.when(j == last)
+            def _():
+                last_chunk((lambda: None,) * 2)
+
+            @pl.when((j >= 2) & (j - 2 < last))
             def _():
                 y_copy(j - 2).wait_recv()
+
+            @pl.when(j - 2 == last)
+            def _():
+                for half in halves:
+                    y_copy(last, half).wait_recv()
 
             @pl.when((j == 2) & (chip != col_at))
             def _():
@@ -316,6 +371,9 @@
 
     def block_at(i):
         return pl.ds(pl.multiple_of(i * RB, RB), RB)
+
+    def m_copy():
+        return pltpu.make_async_remote_copy(m_send, m_in, ms_sem, mr_sem, device_id=to_col)
 
     def cost_min():
         def body(i, _):
@@ -330,10 +388,8 @@
             return 0
         lax.fori_loop(0, blocks, body, 0)
         m_send[...] = gather_rows(jnp.min, range(groups))
-        copy = pltpu.make_async_remote_copy(m_send, m_in, ms_sem, mr_sem, device_id=to_col)
-        copy.start()
-        copy.wait()
-        spread(jnp.minimum(m_send[...], m_in[...]), u_rep, range(groups))
+        m_copy().start()
+        spread(m_send[...], u_rep, range(groups))
 
     def gibbs(scale):
         def body(i, _):
@@ -347,12 +403,14 @@
             part[at] = total
             return 0
         lax.fori_loop(0, blocks, body, 0)
-
-    def row_pass(first_block, last_block, half):
+        m_copy().wait()
+        f_ref[...] = jnp.exp((jnp.minimum(m_send[...], m_in[...]) - m_send[...]) * scale)
+
+    def row_pass(first_block, last_block, first_tile, last_tile):
         def body(i, _):
             at = block_at(i)
-            total = part[at] if half else None
-            for t in range(half * tiles // 2, (half + 1) * tiles // 2):
+            total = part[at] if first_tile else None
+            for t in range(first_tile, last_tile):
                 val = acc[at, lanes(t)] * v_ref[:, lanes(t)]
                 total = val if total is None else total + val
             part[at] = total
@@ -385,13 +443,13 @@
     mid_group, mid_block, mid_col = groups // 2, blocks // 2, cols // 2
 
     def send_rows(slot, half):
-        r_send[slot, half] = gather_rows(jnp.sum, range(half * mid_group, (half + 1) * mid_group))
+        r_send[slot, half] = gather_rows(jnp.sum, range(half * mid_group, (half + 1) * mid_group)) * f_ref[...]
         r_copy(slot, half).start()
 
     def take_rows(slot, half):
         r_copy(slot, half).wait_recv()
         u = p_ref[...] / (r_send[slot, half] + r_in[slot, half])
-        spread(u, u_rep, range(half * mid_group, (half + 1) * mid_group))
+        spread(u * f_ref[...], u_rep, range(half * mid_group, (half + 1) * mid_group))
 
     def send_cols(slot, half, sums):
         for t, val in enumerate(sums):
@@ -445,11 +503,11 @@
             @pl.when(s > 0)
             def _():
                 take_cols(1 - slot, 0)
-                row_pass(0, blocks, 0)
+                row_pass(0, mid_block, 0, tiles // 2)
                 take_cols(1 - slot, 1)
-                row_pass(0, mid_block, 1)
+                row_pass(0, mid_block, tiles // 2, tiles)
                 send_rows(slot, 0)
-                row_pass(mid_block, blocks, 1)
+                row_pass(mid_block, blocks, 0, tiles)
                 send_rows(slot, 1)
 
             take_rows(slot, 0)
@@ -465,10 +523,10 @@
                 sent(1 - slot)
             return 0
         lax.fori_loop(0, SWEEPS, sweep, 0)
-        last = (SWEEPS - 1) % 2
+        final = (SWEEPS - 1) % 2
         for half in range(2):
-            take_cols(last, half)
-        sent(last)
+            take_cols(final, half)
+        sent(final)
         make_plan()
 
     def stage_copy(i):
@@ -489,7 +547,17 @@
                 val = ((a_rows + b_ref[:, lanes(t)]) - 2.0 * acc[at, lanes(t)]) * stage[g % 2, :, lanes(t)]
                 out = val if out is None else out + val
             return total + out
-        loss_out[...] = lax.fori_loop(0, groups, body, jnp.zeros((SUB, LANES), F32))
+        total = lax.fori_loop(0, groups, body, jnp.zeros((SUB, LANES), F32))
+        c_send[0, 0, :, lanes(0)] = jnp.sum(total, axis=0, keepdims=True)
+        for copy in c_copies(0, 0):
+            copy.start()
+        for copy in c_copies(0, 0):
+            copy.wait()
+        total = (c_send[0, 0] + c_in[0, 0, 0]) + (c_in[0, 0, 1] + c_in[0, 0, 2])
+        m_send[...] = jnp.broadcast_to(total[:, lanes(0)], (SUB, LANES))
+        m_copy().start()
+        m_copy().wait()
+        loss_out[...] = m_send[...] + m_in[...]
 
     for j in range(chunks):
         pltpu.make_async_copy(t0_ref.at[:, j * W:(j + 1) * W], panel.at[j, rows_of(row_at)], io_sem).start()
@@ -590,12 +658,13 @@
                 pltpu.VMEM((SUB, cols), F32),
                 pltpu.VMEM((SUB, LANES), F32),
                 pltpu.VMEM((SUB, LANES), F32),
+                pltpu.VMEM((SUB, LANES), F32),
                 pltpu.VMEM((2, 2, SUB, LANES), F32),
                 pltpu.VMEM((2, 2, SUB, LANES), F32),
                 pltpu.VMEM((2, 2, 1, cols // 2), F32),
                 pltpu.VMEM((2, 2, 3, 1, cols // 2), F32),
                 pltpu.VMEM((2, SUB, cols), F32),
-                *[dma((chunks,))] * 8,
+                *[dma((chunks + 1,))] * 8,
                 dma((2,)), dma((2,)), dma, dma, dma((2, 2)), dma((2, 2)), dma((2, 2, 3)), dma((2, 2, 3)),
                 dma, dma((2,)),
                 *[dma((c2_height // W,))] * 8,
@@ -603,6 +672,6 @@
             ],
             compiler_params=pltpu.CompilerParams(collective_id=0, has_side_effects=True, vmem_limit_bytes=67043328),
         )(c1_blk.astype(BF16), t0_blk.astype(BF16), c2_blk.astype(BF16), packed_rows(row_term), col_term[None], packed_rows(p_blk), q_blk[None], eps_blk)
-        return plan, lax.psum(jnp.sum(loss_part), ("rows", "cols")).reshape(1)
+        return plan, jnp.sum(loss_part[0]).reshape(1)
 
     return jax.shard_map(local_fn, mesh=mesh, in_specs=(grid_spec, grid_spec, grid_spec, P(("pairs", "rows")), P(("pairs", "cols")), P("pairs")), out_specs=(grid_spec, P("pairs")), check_vma=False)

time: 2430 us -> 2380 us (0.979)
  Pallas kernels: 2330 us -> 2300 us
    pallas_call x1, Pallas kernels: 2330 us -> 2300 us  [local_fn(): pl.pallas_call(functools.partial(outer_kernel, steps), out_shape=(jax.Sha...]
where the time goes in v3:
time: 2380 us
  Pallas kernels  2300 us (97%)
  other arithmetic  45.2 us (2%)
    pallas_call x1, Pallas kernels, local_fn(): pl.pallas_call(functools.partial(outer_kernel, steps), out_shape=(jax.Sha...  2300 us

profile of v3, /device:TPU:0, one launch (start us, length us, event | category | flops | bytes accessed | tf_op | source)
XLA Modules:
  0.0 2377.7 jit_solution(11029806837945594391)
XLA Ops:
  0.6 0.7 reshape.18
  1.3 10.0 all-gather
  11.3 0.1 dynamic_slice.6
  11.4 4.4 all_gather.7
  15.8 0.8 reshape.16
  16.5 0.1 copy.11
  16.6 0.6 pad.8.p_ref
  17.2 6.0 multiply_reduce_fusion.1
  23.2 0.1 reshape.15
  23.3 0.1 copy.10
  23.3 0.6 pad.7.a_ref
  24.0 8.2 convert_element_type.10.t0_ref
  32.2 29.7 %multiply_reduce_fusion = (f32[4096]{0:T(1024)}, bf16[2048,4096]{1,0:T(8,128)(2,1)}) fusion(f32[2048,4096]{1,0:T(8,128)} %param.7, f32[2048]{0:T(1024)S(1)} %dynamic_slice.7), kind=kLoop, calls=%fused_computation | loop fusion | flops 33550336 | bytes 50356224 | tf_op jit(solution)/shard_map/reduce_sum | solution.py:632
  61.9 2303.6 %shard_map.77 = (f32[768,4096]{1,0:T(8,128)}, f32[8,128]{1,0:T(8,128)}, bf16[16,8192,256]{2,1,0:T(8,128)(2,1)}, bf16[16,4096,256]{2,1,0:T(8,128)(2,1)}) custom-call(bf16[768,1536]{1,0:T(8,128)(2,1)} %get-tuple-element.9.c1_blk, bf16[768,4096]{1,0:T(8,128)(2,1)} %convert_element_type.10.t0_ref, bf16[2048,4096]{1,0:T(8,128)(2,1)} %get-tuple-element.7.c2_blk, ...), custom_call_target="tpu_custom_call" | custom-call | tf_op jit(solution)/shard_map/pallas_call | solution.py:638
  2365.5 1.3 slice_reduce_fusion
  2366.8 10.9 copy.13
  (1 shorter events, 0.0 us)

commit v4 on v3

--- a/solution.py
+++ b/solution.py
@@ -18,12 +18,12 @@
 BF16 = jnp.bfloat16
 
 
-def outer_kernel(steps, c1_blk, t0_ref, c2_blk, a_ref, b_part, p_ref, q_ref, eps_ref, t_out, loss_out, c2_ref, c2_turn,
-                 acc, panel, c1_ref, lead_in, c2_own, c2_in, turn_in, turn_out, b_ref, v_ref, a_rep, u_rep, part, c_part, f_ref,
+def outer_kernel(steps, c1_blk, t0_ref, c2_blk, c2_wide, a_ref, q_pack, p_ref, q_ref, eps_ref, t_out, loss_out, c2_ref, c2_turn,
+                 acc, panel, c1_ref, lead_in, c2_own, c2_in, turn_in, turn_out, q_in, q_rows, b_ref, v_ref, a_rep, u_rep, part, c_part, f_ref,
                  m_send, m_in, r_send, r_in, c_send, c_in, stage,
                  x_send, x_recv, d_send, d_recv, f_send, f_recv, y_send, y_recv,
                  own_sem, in_sem, ms_sem, mr_sem, rs_sem, rr_sem, cs_sem, cr_sem, io_sem, st_sem,
-                 xs_sem, xr_sem, ts_sem, tr_sem, fs_sem, fr_sem, us_sem, ur_sem, bs_sem, br_sem, os_sem, or_sem, turn_sem):
+                 xs_sem, xr_sem, ts_sem, tr_sem, fs_sem, fr_sem, us_sem, ur_sem, bs_sem, br_sem, os_sem, or_sem, qs_sem, qr_sem, turn_sem):
     rows, cols = acc.shape
     chunks = cols // W
     row_at = lax.axis_index("rows")
@@ -172,7 +172,9 @@
             f_copy(last, half).wait_send()
             y_copy(last, half).wait_send()
 
-    def cost():
+    plan_out = pltpu.make_async_copy(acc, t_out, io_sem)
+
+    def cost(r):
         for i in range(2):
             c2_start(col_at, i, c2_own, own_sem)
             c2_start(1 - col_at, i, c2_in, in_sem)
@@ -185,6 +187,10 @@
 
         def step(j, _):
             take_chunk(j)
+
+            @pl.when((j == 1) & (r == steps - 1))
+            def _():
+                plan_out.wait()
 
             @pl.when(j == 1)
             def _():
@@ -271,6 +277,28 @@
             pltpu.make_async_copy(turn_out.at[d - 1], c2_ref.at[k, quad_rows(far * cols, (k + d) % chunks)], turn_sem.at[1]).start()
         pltpu.make_async_copy(turn_out, many(c2_ref, HALF - 1), turn_sem.at[1]).wait()
 
+    def col_terms(j):
+        count = held // SUB // chunks
+
+        def wide_copy(n):
+            src = c2_wide.at[pl.ds(pl.multiple_of((j * count + n) * SUB, SUB), SUB)]
+            return pltpu.make_async_copy(src, stage.at[n % 2], st_sem.at[n % 2])
+        wide_copy(0).start()
+
+        def body(n, _):
+            @pl.when(n + 1 < count)
+            def _():
+                wide_copy(n + 1).start()
+            g = j * count + n
+            weight = jnp.sum(jnp.where(lane == g % LANES, q_rows[g // LANES], 0.0), axis=1, keepdims=True)
+            weight = jnp.broadcast_to(weight, (SUB, LANES))
+            wide_copy(n).wait()
+            for t in range(tiles):
+                val = stage[n % 2, :, lanes(t)]
+                c_part[:, lanes(t)] = c_part[:, lanes(t)] + val * val * weight
+            return 0
+        lax.fori_loop(0, count, body, 0)
+
     def first_cost(own_block, c1_copy):
         own_block.wait_recv()
         for i in range(2):
@@ -304,6 +332,10 @@
             @pl.when(j == last)
             def _():
                 last_chunk((lambda: None,) * 2)
+
+            @pl.when(j < chunks)
+            def _():
+                col_terms(j)
 
             @pl.when((j >= 2) & (j - 2 < last))
             def _():
@@ -335,6 +367,11 @@
 
         for i in range(2):
             c2_start(far, i, c2_in, in_sem)
+        for half in range(2):
+            for t in range(tiles // 2):
+                c_send[1, half, :, lanes(t)] = jnp.sum(c_part[:, lanes(half * tiles // 2 + t)], axis=0, keepdims=True)
+            for copy in c_copies(1, half):
+                copy.start()
 
         def rest(i, _):
             @pl.when(chip == col_at)
@@ -346,6 +383,11 @@
                 product(far, i, lead_at(i), c2_in, in_sem)
             return 0
         lax.fori_loop(0, chunks, rest, 0)
+        for half in range(2):
+            for copy in c_copies(1, half):
+                copy.wait()
+            total = (c_send[1, half] + c_in[1, half, 0]) + (c_in[1, half, 1] + c_in[1, half, 2])
+            b_ref[:, half * mid_col:(half + 1) * mid_col] = total
         drain_chunks()
         own_block.wait_send()
         c1_copy.wait_send()
@@ -470,15 +512,13 @@
             for copy in c_copies(slot, half):
                 copy.wait_send()
 
-    def make_plan():
+    def form_chunks(form):
         def chunk(j, _):
             def body(i, _):
                 at = block_at(i)
                 for t in range(W // LANES):
                     where = pl.ds(pl.multiple_of(j * W + t * LANES, LANES), LANES)
-                    val = (u_rep[at] * acc[at, where]) * v_ref[:, where]
-                    acc[at, where] = val
-                    panel[j, pl.ds(pl.multiple_of(row_at * rows + i * RB, RB), RB), lanes(t)] = val.astype(BF16)
+                    panel[j, pl.ds(pl.multiple_of(row_at * rows + i * RB, RB), RB), lanes(t)] = form(at, where).astype(BF16)
                 return 0
             lax.fori_loop(0, blocks, body, 0)
 
@@ -487,6 +527,11 @@
                 issue(j)
             return 0
         lax.fori_loop(0, chunks, chunk, 0)
+
+    def plan_at(at, where):
+        val = (u_rep[at] * acc[at, where]) * v_ref[:, where]
+        acc[at, where] = val
+        return val
 
     def sinkhorn(r):
         cost_min()
@@ -527,7 +572,7 @@
         for half in range(2):
             take_cols(final, half)
         sent(final)
-        make_plan()
+        form_chunks(plan_at)
 
     def stage_copy(i):
         return pltpu.make_async_copy(t_out.at[pl.ds(pl.multiple_of(i * SUB, SUB), SUB)], stage.at[i % 2], st_sem.at[i % 2])
@@ -559,9 +604,10 @@
         m_copy().wait()
         loss_out[...] = m_send[...] + m_in[...]
 
-    for j in range(chunks):
-        pltpu.make_async_copy(t0_ref.at[:, j * W:(j + 1) * W], panel.at[j, rows_of(row_at)], io_sem).start()
-    first_plan = pltpu.make_async_copy(panel.at[:, rows_of(row_at)], panel.at[:, rows_of(row_at)], io_sem)
+    first_plan = pltpu.make_async_copy(t0_ref, acc, io_sem)
+    first_plan.start()
+    q_copy = pltpu.make_async_remote_copy(q_pack, q_in, qs_sem, qr_sem, device_id=to_col)
+    q_copy.start()
     width = c1_blk.shape[1]
     c1_at = c1_ref.at[:, pl.ds(pl.multiple_of(col_at * width, width), width)]
     c1_here = pltpu.make_async_copy(c1_blk, c1_at, st_sem.at[0])
@@ -574,25 +620,25 @@
         piece = c2_blk.at[:, n * W:(n + 1) * W]
         pltpu.make_async_remote_copy(piece, own_rows.at[n], bs_sem, br_sem, device_id=to_sib).start()
     first_plan.wait()
-    for j in range(AHEAD):
-        issue(j)
+    form_chunks(lambda at, where: acc[at, where])
 
     m_send[...] = a_ref[...]
-    a_copy = pltpu.make_async_remote_copy(m_send, m_in, ms_sem, mr_sem, device_id=to_col)
-    a_copy.start()
-    for half in range(2):
-        c_send[0, half] = b_part[:, half * mid_col:(half + 1) * mid_col]
-        for copy in c_copies(0, half):
-            copy.start()
-    a_copy.wait()
+    m_copy().start()
+    q_copy.wait()
+    for n in range(q_rows.shape[0]):
+        piece = pl.ds(pl.multiple_of((core * q_rows.shape[0] + n) * LANES, LANES), LANES)
+
+        @pl.when(chip == col_at)
+        def _():
+            q_rows[n] = q_pack[:, piece]
+
+        @pl.when(chip != col_at)
+        def _():
+            q_rows[n] = q_in[:, piece]
+    c_part[...] = jnp.zeros_like(c_part)
+    m_copy().wait()
     spread(m_send[...] + m_in[...], a_rep, range(groups))
-    for half in range(2):
-        for copy in c_copies(0, half):
-            copy.wait()
-        total = (c_send[0, half] + c_in[0, half, 0]) + (c_in[0, half, 1] + c_in[0, half, 2])
-        b_ref[:, half * mid_col:(half + 1) * mid_col] = total
     c1_here.wait()
-    plan_out = pltpu.make_async_copy(acc, t_out, io_sem)
     first_cost(own_block, c1_copy)
 
     def outer(r, _):
@@ -601,8 +647,7 @@
         @pl.when(r == steps - 1)
         def _():
             plan_out.start()
-            plan_out.wait()
-        cost()
+        cost(r)
         return 0
     lax.fori_loop(0, steps, outer, 0)
     loss()
@@ -618,18 +663,15 @@
 
     def local_fn(c1_blk, c2_blk, t0_blk, p_blk, q_blk, eps_blk):
         col_pos = lax.axis_index("cols")
-        row_pos = lax.axis_index("rows")
         c1_width = c1_blk.shape[1]
         c2_height = c2_blk.shape[0]
         rows, cols = t0_blk.shape
         chunks = cols // W
         steps = eps_blk.shape[0]
         p_full = lax.all_gather(p_blk, "rows", tiled=True)
-        q_full = lax.all_gather(q_blk, "cols", tiled=True)
         p_piece = lax.dynamic_slice_in_dim(p_full, col_pos * c1_width, c1_width)
-        q_piece = lax.dynamic_slice_in_dim(q_full, row_pos * c2_height, c2_height)
         row_term = jnp.sum(c1_blk * c1_blk * p_piece[None, :], axis=1)
-        col_term = jnp.sum(c2_blk * c2_blk * q_piece[:, None], axis=0)
+        q_pack = q_blk.reshape(cols // SUB, SUB).T
 
         vmem = pl.BlockSpec(memory_space=pltpu.VMEM)
         smem = pl.BlockSpec(memory_space=pltpu.SMEM)
@@ -641,7 +683,7 @@
                 jax.ShapeDtypeStruct((rows, cols), F32), jax.ShapeDtypeStruct((SUB, LANES), F32),
                 jax.ShapeDtypeStruct((chunks, 2 * cols, W), BF16), jax.ShapeDtypeStruct((chunks, cols, W), BF16),
             ),
-            in_specs=[hbm, hbm, hbm, vmem, vmem, vmem, vmem, smem],
+            in_specs=[hbm, hbm, hbm, hbm, vmem, vmem, vmem, vmem, smem],
             out_specs=(hbm, vmem, hbm, hbm),
             scratch_shapes=[
                 pltpu.VMEM((rows, cols), F32),
@@ -652,6 +694,8 @@
                 pltpu.VMEM((2, W, cols), BF16),
                 pltpu.VMEM((HALF - 1, W, W), BF16),
                 pltpu.VMEM((HALF - 1, W, W), BF16),
+                pltpu.VMEM((SUB, cols // SUB), F32),
+                pltpu.VMEM((c2_height // SUB // LANES, SUB, LANES), F32),
                 pltpu.VMEM((1, cols), F32),
                 pltpu.VMEM((1, cols), F32),
                 *[pltpu.VMEM((rows, LANES), F32)] * 3,
@@ -668,10 +712,10 @@
                 dma((2,)), dma((2,)), dma, dma, dma((2, 2)), dma((2, 2)), dma((2, 2, 3)), dma((2, 2, 3)),
                 dma, dma((2,)),
                 *[dma((c2_height // W,))] * 8,
-                dma, dma, dma, dma, dma((2,)),
+                dma, dma, dma, dma, dma, dma, dma((2,)),
             ],
             compiler_params=pltpu.CompilerParams(collective_id=0, has_side_effects=True, vmem_limit_bytes=67043328),
-        )(c1_blk.astype(BF16), t0_blk.astype(BF16), c2_blk.astype(BF16), packed_rows(row_term), col_term[None], packed_rows(p_blk), q_blk[None], eps_blk)
+        )(c1_blk.astype(BF16), t0_blk, c2_blk.astype(BF16), c2_blk, packed_rows(row_term), q_pack, packed_rows(p_blk), q_blk[None], eps_blk)
         return plan, jnp.sum(loss_part[0]).reshape(1)
 
     return jax.shard_map(local_fn, mesh=mesh, in_specs=(grid_spec, grid_spec, grid_spec, P(("pairs", "rows")), P(("pairs", "cols")), P("pairs")), out_specs=(grid_spec, P("pairs")), check_vma=False)

time: 2380 us -> 2360 us (level)
    reduce_sum x1 -> x0, other arithmetic: 29.7 us -> none  [local_fn(): col_term = jnp.sum(c2_blk * c2_blk * q_piece[:, None], axis=0)]
where the time goes in v4:
time: 2360 us; the launch traced here: 2350 us
  Pallas kernels  2300 us (97%)
  other arithmetic  24.5 us (1%)
    pallas_call x1, Pallas kernels, local_fn(): pl.pallas_call(functools.partial(outer_kernel, steps), out_shape=(jax.Sha...  2300 us

profile of v4, /device:TPU:0, one launch (start us, length us, event | category | flops | bytes accessed | tf_op | source)
XLA Modules:
  0.0 2354.5 jit_solution(5995871604160949080)
XLA Ops:
  0.6 0.7 reshape.21
  1.3 10.0 all-gather
  11.3 0.1 dynamic_slice.3
  11.4 0.8 reshape.19
  12.1 0.1 copy.13
  12.2 0.6 pad.8.p_ref
  12.8 0.9 reshape.18
  13.7 0.7 copy.12
  14.4 5.9 multiply_reduce_fusion
  20.3 0.1 reshape.17
  20.4 0.1 copy.11
  20.4 0.6 pad.7.a_ref
  21.1 17.3 convert_element_type.7.c2_blk
  38.4 2303.9 %shard_map.77 = (f32[768,4096]{1,0:T(8,128)}, f32[8,128]{1,0:T(8,128)}, bf16[16,8192,256]{2,1,0:T(8,128)(2,1)}, bf16[16,4096,256]{2,1,0:T(8,128)(2,1)}) custom-call(bf16[768,1536]{1,0:T(8,128)(2,1)} %get-tuple-element.7.c1_blk, f32[768,4096]{1,0:T(8,128)} %t0_ref.1, bf16[2048,4096]{1,0:T(8,128)(2,1)} %convert_element_type.7.c2_blk, f32[2048,4096]{1,0:T(8,128)} %c2_wide.1, ...), custom_call_target="tpu_custom_call" | custom-call | tf_op jit(solution)/shard_map/pallas_call | solution.py:680
  2342.3 1.3 slice_reduce_fusion
  2343.6 10.9 copy.15
